TPU v7x, 16 devices: a whole 2x2x2 slice. The times are simulated.
16 devices in a mesh: att: 4 (over z, y), emb: 4 (over x, core).
Axes of the slice: x: 2, y: 2, z: 2, core: 2. Of those that a mesh axis runs over, the one named last changes fastest.
Arguments:
- w_qkv: float32 [4, 3, 2048, 2048], P(None, None, 'emb', 'att')
- w_out: float32 [4, 2048, 2048], P(None, 'att', 'emb')
- x_in: bfloat16 [4, 2048, 2048], P(None, None, 'emb')
- dy_qkv: bfloat16 [4, 3, 2048, 2048], P(None, None, None, 'att')
- x_attn: bfloat16 [4, 2048, 2048], P(None, None, 'att')
- dy_out: bfloat16 [4, 2048, 2048], P(None, None, 'emb')
- r_qkv: float32 [4, 3, 2048], P(None, None, 'emb')
- c_qkv: float32 [4, 3, 2048], P(None, None, 'att')
- r_out: float32 [4, 2048], P(None, 'att')
- c_out: float32 [4, 2048], P(None, 'emb')
- hyper_params: float32 [3], replicated
Outputs:
- output 1: float32 [4, 3, 2048, 2048], P(None, None, 'emb', 'att')
- output 2: float32 [4, 2048, 2048], P(None, 'att', 'emb')
- output 3: float32 [4, 3, 2048], P(None, None, 'emb')
- output 4: float32 [4, 3, 2048], P(None, None, 'att')
- output 5: float32 [4, 2048], P(None, 'att')
- output 6: float32 [4, 2048], P(None, 'emb')
All inputs are finite; a program needn't handle non-finite values.
Results may differ from a plain program's by a relative error of at most 0.001.
Values are sent between devices in bfloat16 or wider.
A program may use at most 1 GiB of HBM per device.

v0:
```python
import jax
import jax.numpy as jnp
from jax import lax
from jax.sharding import PartitionSpec as P

EPS_SQUARE = 1e-30
EPS_SCALE = 1e-3


def factored_step(w_grad, weight, row_old, col_old, hyper_params, m_axis, n_axis, m_total, n_total):
    beta_two = hyper_params[0]
    rel_step = hyper_params[1]
    clip_limit = hyper_params[2]
    q_sq = w_grad * w_grad + EPS_SQUARE
    row_part = jnp.sum(q_sq, axis=2)
    col_part = jnp.sum(q_sq, axis=1)
    lead_flag = (lax.axis_index(n_axis) == 0).astype(jnp.float32)
    scalar_part = jnp.stack(
        [jnp.sum(col_part, axis=1), jnp.sum(weight * weight, axis=(1, 2)), lead_flag * jnp.sum(row_old, axis=1)],
        axis=1,
    )
    row_sum = lax.psum(row_part, n_axis)
    col_sum = lax.psum(col_part, m_axis)
    scalar_sum = lax.psum(scalar_part, (m_axis, n_axis))
    n_elems = m_total * n_total
    row_new = beta_two * row_old + (1.0 - beta_two) * (row_sum / n_total)
    col_new = beta_two * col_old + (1.0 - beta_two) * (col_sum / m_total)
    mean_row = beta_two * scalar_sum[:, 2] / m_total + (1.0 - beta_two) * scalar_sum[:, 0] / n_elems
    row_factor = lax.rsqrt(row_new / mean_row[:, None])
    col_factor = lax.rsqrt(col_new)
    update = w_grad * row_factor[:, :, None] * col_factor[:, None, :]
    u_sum = lax.psum(jnp.sum(update * update, axis=(1, 2)), (m_axis, n_axis))
    rms_u = jnp.sqrt(u_sum / n_elems)
    rms_w = jnp.sqrt(scalar_sum[:, 1] / n_elems)
    step_size = rel_step * jnp.maximum(EPS_SCALE, rms_w) / jnp.maximum(1.0, rms_u / clip_limit)
    return weight - step_size[:, None, None] * update, row_new, col_new


def solution(mesh):
    emb_size = mesh.shape["emb"]
    att_size = mesh.shape["att"]
    in_specs = (
        P(None, None, "emb", "att"),
        P(None, "att", "emb"),
        P(None, None, "emb"),
        P(None, None, None, "att"),
        P(None, None, "att"),
        P(None, None, "emb"),
        P(None, None, "emb"),
        P(None, None, "att"),
        P(None, "att"),
        P(None, "emb"),
        P(),
    )
    out_specs = (
        P(None, None, "emb", "att"),
        P(None, "att", "emb"),
        P(None, None, "emb"),
        P(None, None, "att"),
        P(None, "att"),
        P(None, "emb"),
    )

    def local_run(w_qkv, w_out, x_in, dy_qkv, x_attn, dy_out, r_qkv, c_qkv, r_out, c_out, hyper_params):
        d_model = x_in.shape[2] * emb_size
        inner_dim = x_attn.shape[2] * att_size
        per_layer = []
        for layer_idx in range(w_qkv.shape[0]):
            g_qkv = jnp.einsum("td,ktn->kdn", x_in[layer_idx], dy_qkv[layer_idx], preferred_element_type=jnp.float32)
            new_qkv = factored_step(
                g_qkv, w_qkv[layer_idx], r_qkv[layer_idx], c_qkv[layer_idx], hyper_params, "emb", "att", d_model, inner_dim
            )
            g_out = jnp.einsum("ti,td->id", x_attn[layer_idx], dy_out[layer_idx], preferred_element_type=jnp.float32)
            new_out = factored_step(
                g_out[None], w_out[layer_idx][None], r_out[layer_idx][None], c_out[layer_idx][None],
                hyper_params, "att", "emb", inner_dim, d_model
            )
            per_layer.append((new_qkv[0], new_out[0][0], new_qkv[1], new_qkv[2], new_out[1][0], new_out[2][0]))
        return tuple(jnp.stack([layer_out[out_slot] for layer_out in per_layer]) for out_slot in range(6))

    return jax.shard_map(local_run, mesh=mesh, in_specs=in_specs, out_specs=out_specs, check_vma=False)
```

profile of v0, /device:TPU:0, one launch (start us, length us, event | category | flops | bytes accessed | tf_op | source)
XLA Modules:
  0.0 325.3 jit_solution(14640504072774040870)
XLA Ops:
  2.7 1.5 slice_reduce_fusion.3
  6.8 3.5 %multiply_reduce_fusion.11 = (f32[]{:T(128)}, f32[]{:T(128)}, f32[]{:T(128)}, f32[]{:T(128)}) fusion(f32[4,512,512]{2,1,0:T(8,128)} %param.12), kind=kLoop, calls=%fused_computation.100 | loop fusion | flops 2097148 | bytes 4194320 | tf_op jit(solution)/shard_map/reduce_sum | solution.py:19
  10.5 4.4 %fusion.64 = (f32[512]{0:T(512)S(1)}, f32[512]{0:T(512)S(1)}, f32[]{:T(128)}, f32[512,512]{1,0:T(8,128)S(1)}) fusion(bf16[4,2048,512]{2,1,0:T(8,128)(2,1)} %param.16, bf16[4,2048,512]{2,1,0:T(8,128)(2,1)} %param.15), kind=kOutput, calls=%fused_computation.106 | convolution fusion | flops 1075051520 | bytes 5246980 | tf_op jit(solution)/shard_map/ti,td->id/dot_general | solution.py:73
  16.2 3.6 %fusion.61 = (f32[512]{0:T(512)S(1)}, f32[512]{0:T(512)S(1)}, f32[]{:T(128)}, f32[512,512]{1,0:T(8,128)S(1)}) fusion(bf16[4,2048,512]{2,1,0:T(8,128)(2,1)S(1)} %copy-done.13, bf16[4,2048,512]{2,1,0:T(8,128)(2,1)} %param.15), kind=kOutput, calls=%fused_computation.103 | convolution fusion | flops 1075051520 | bytes 5246980 | tf_op jit(solution)/shard_map/ti,td->id/dot_general | solution.py:73
  21.2 2.9 fusion.70
  25.5 2.0 fusion.67
  28.8 34.8 %all-reduce.1 = (f32[1,3]{1,0:T(1,128)S(1)}, f32[1,3]{1,0:T(1,128)S(1)}, f32[1,3]{1,0:T(1,128)S(1)}, f32[1,3]{1,0:T(1,128)S(1)}) all-reduce(f32[1,3]{1,0:T(1,128)S(1)} %pad_maximum_fusion.13, f32[1,3]{1,0:T(1,128)S(1)} %pad_maximum_fusion.12, f32[1,3]{1,0:T(1,128)S(1)} %pad_maximum_fusion.11, ...), channel_id=1, replica_groups=mesh['att'=4,'emb'=4] {'att','emb'}, use_global_device_ids=true, to_apply=%region_73.0 | all-reduce | flops 12 | bytes 96 | tf_op jit(solution)/shard_map/psum | solution.py:24
  78.0 9.0 %fusion.24 = (f32[3,512]{1,0:T(4,128)S(1)}, f32[3,512]{1,0:T(4,128)S(1)}, f32[3]{0:T(128)S(1)}, f32[3,512,512]{2,1,0:T(8,128)}) fusion(bf16[4,2048,512]{2,1,0:T(8,128)(2,1)} %param.13, bf16[4,3,2048,512]{3,2,1,0:T(8,128)(2,1)} %param.14), kind=kOutput, calls=%fused_computation.46 | convolution fusion | flops 3225154560 | bytes 11546636 | tf_op jit(solution)/shard_map/td,ktn->kdn/dot_general | solution.py:69
  87.0 8.9 %fusion.21 = (f32[3,512]{1,0:T(4,128)S(1)}, f32[3,512]{1,0:T(4,128)S(1)}, f32[3]{0:T(128)S(1)}, f32[3,512,512]{2,1,0:T(8,128)}) fusion(bf16[4,2048,512]{2,1,0:T(8,128)(2,1)} %param.13, bf16[4,3,2048,512]{3,2,1,0:T(8,128)(2,1)} %param.14), kind=kOutput, calls=%fused_computation.43 | convolution fusion | flops 3225154560 | bytes 11546636 | tf_op jit(solution)/shard_map/td,ktn->kdn/dot_general | solution.py:69
  96.0 7.1 %fusion.30 = (f32[3,512]{1,0:T(4,128)S(1)}, f32[3,512]{1,0:T(4,128)S(1)}, f32[3]{0:T(128)S(1)}, f32[3,512,512]{2,1,0:T(8,128)}) fusion(bf16[4,2048,512]{2,1,0:T(8,128)(2,1)} %param.13, bf16[4,3,2048,512]{3,2,1,0:T(8,128)(2,1)S(1)} %bitcast.341), kind=kOutput, calls=%fused_computation.52 | convolution fusion | flops 3225154560 | bytes 11546636 | tf_op jit(solution)/shard_map/td,ktn->kdn/dot_general | solution.py:69
  103.1 7.4 %fusion.27 = (f32[3,512]{1,0:T(4,128)S(1)}, f32[3,512]{1,0:T(4,128)S(1)}, f32[3]{0:T(128)S(1)}, f32[3,512,512]{2,1,0:T(8,128)}) fusion(bf16[4,2048,512]{2,1,0:T(8,128)(2,1)} %param.13, bf16[4,3,2048,512]{3,2,1,0:T(8,128)(2,1)S(1)} %bitcast.341), kind=kOutput, calls=%fused_computation.49 | convolution fusion | flops 3225154560 | bytes 11546636 | tf_op jit(solution)/shard_map/td,ktn->kdn/dot_general | solution.py:69
  110.5 16.5 %all-reduce.5 = (f32[3,512]{1,0:T(4,128)S(1)}, f32[3,512]{1,0:T(4,128)S(1)}, f32[3,512]{1,0:T(4,128)S(1)}, f32[3,512]{1,0:T(4,128)S(1)}, f32[1,512]{1,0:T(1,128)...) all-reduce(f32[3,512]{1,0:T(4,128)S(1)} %get-tuple-element.31, ...), channel_id=1, replica_groups=mesh['att'=4,'emb'=4] {'att'}, use_global_device_ids=true, to_apply=%region_35.0 | all-reduce | flops 8192 | bytes 65536 | tf_op jit(solution)/shard_map/psum | solution.py:22
  127.1 10.5 %all-reduce.4 = (f32[3,512]{1,0:T(4,128)S(1)}, f32[3,512]{1,0:T(4,128)S(1)}, f32[3,512]{1,0:T(4,128)S(1)}, f32[3,512]{1,0:T(4,128)S(1)}, f32[1,512]{1,0:T(1,128)...) all-reduce(f32[3,512]{1,0:T(4,128)S(1)} %get-tuple-element.32, ...), channel_id=1, replica_groups=mesh['att'=4,'emb'=4] {'emb'}, use_global_device_ids=true, to_apply=%region_37.0 | all-reduce | flops 8192 | bytes 65536 | tf_op jit(solution)/shard_map/psum | solution.py:23
  140.2 2.2 multiply_reduce_fusion.4
  145.3 32.3 %all-reduce = (f32[1]{0:T(128)}, f32[1]{0:T(128)}, f32[1]{0:T(128)}, f32[1]{0:T(128)}) all-reduce(f32[1]{0:T(128)} %bitcast.117, f32[1]{0:T(128)} %bitcast.101, f32[1]{0:T(128)} %bitcast.85, f32[1]{0:T(128)} %bitcast.69), channel_id=1, replica_groups=mesh['att'=4,'emb'=4] {'att','emb'}, use_global_device_ids=true, to_apply=%region_79.0 | all-reduce | flops 4 | bytes 32 | tf_op jit(solution)/shard_map/psum | solution.py:32
  183.0 2.7 bitcast_subtract_fusion.7
  187.2 2.5 pad_maximum_fusion.1
  191.6 9.7 %fusion.104 = (f32[1,3,512,512]{3,2,1,0:T(8,128)}, f32[1,3,512,512]{3,2,1,0:T(8,128)}, f32[1,3,512,512]{3,2,1,0:T(8,128)}, f32[1,3,512,512]{3,2,1,0:T(8,128)}) fusion(f32[4,3,512,512]{3,2,1,0:T(8,128)} %param.11), kind=kLoop, calls=%fused_computation.202 | loop fusion | bytes 25165824 | tf_op jit(solution)/shard_map/slice | solution.py:71
  201.3 2.4 copy.57
  205.4 2.4 copy.65
  208.2 3.5 %copy.61 = f32[1,3,512,512]{2,3,1,0:T(8,128)} copy(f32[1,3,512,512]{3,2,1,0:T(8,128)} %get-tuple-element.104) | data formatting | bytes 6291456
  211.7 2.3 fusion.17
  214.0 3.5 %copy.69 = f32[1,3,512,512]{2,3,1,0:T(8,128)} copy(f32[1,3,512,512]{3,2,1,0:T(8,128)} %get-tuple-element.105) | data formatting | bytes 6291456
  217.6 2.3 fusion.13
  219.9 33.1 %all-reduce.3 = (f32[3,3]{0,1:T(4,128)S(1)}, f32[3,3]{0,1:T(4,128)S(1)}, f32[3,3]{0,1:T(4,128)S(1)}, f32[3,3]{0,1:T(4,128)S(1)}) all-reduce(f32[3,3]{0,1:T(4,128)S(1)} %pad_maximum_fusion.9, f32[3,3]{0,1:T(4,128)S(1)} %pad_maximum_fusion.8, f32[3,3]{0,1:T(4,128)S(1)} %pad_maximum_fusion.7, ...), channel_id=1, replica_groups=mesh['att'=4,'emb'=4] {'emb','att'}, use_global_device_ids=true, to_apply=%region_33.0 | all-reduce | flops 36 | bytes 288 | tf_op jit(solution)/shard_map/psum | solution.py:24
  256.7 2.8 multiply_reduce_fusion.3
  263.1 32.6 %all-reduce.2 = (f32[3]{0:T(128)S(1)}, f32[3]{0:T(128)S(1)}, f32[3]{0:T(128)S(1)}, f32[3]{0:T(128)S(1)}) all-reduce(f32[3]{0:T(128)S(1)} %multiply_reduce_fusion, f32[3]{0:T(128)S(1)} %multiply_reduce_fusion.1, f32[3]{0:T(128)S(1)} %multiply_reduce_fusion.2, ...), channel_id=1, replica_groups=mesh['att'=4,'emb'=4] {'emb','att'}, use_global_device_ids=true, to_apply=%region_39.0 | all-reduce | flops 12 | bytes 96 | tf_op jit(solution)/shard_map/psum | solution.py:32
  296.9 3.5 %fusion.18 = f32[1,3,512,512]{2,3,1,0:T(8,128)S(1)} fusion(f32[1,3,512,512]{2,3,1,0:T(8,128)} %copy-done.1, f32[3,512,512]{2,1,0:T(8,128)} %get-tuple-element.167, f32[3]{0:T(128)S(1)} %bitcast_divide_fusion.3, f32[3,512]{1,0:T(4,128)S(1)} %get-tuple-element.118, f32[3,512]{1,0:T(4,128)S(1)} %get-tuple-element.126), kind=kLoop, calls=%fused_computation.27 | loop fusion | flops 3145728 | bytes 9449484 | tf_op jit(solution)/shard_map/stack | solution.py:79
  302.4 1.5 bitcast_divide_fusion.1
  304.4 1.9 bitcast_divide_fusion
  307.2 5.0 %pad_maximum_fusion = f32[4,3,512,512]{2,3,1,0:T(8,128)} fusion(f32[1,3,512,512]{2,3,1,0:T(8,128)S(1)} %fusion.12, f32[1,3,512,512]{2,3,1,0:T(8,128)S(1)} %fusion.14, f32[1,3,512,512]{2,3,1,0:T(8,128)S(1)} %fusion.16, f32[1,3,512,512]{2,3,1,0:T(8,128)S(1)} %fusion.18), kind=kLoop, calls=%fused_computation | loop fusion | flops 9437184 | bytes 25165824 | tf_op jit(solution)/shard_map/stack | solution.py:79
  312.3 12.6 %copy.54 = f32[4,3,512,512]{3,2,1,0:T(8,128)} copy(f32[4,3,512,512]{2,3,1,0:T(8,128)} %pad_maximum_fusion) | data formatting | bytes 25165824
  (90 shorter events, 31.2 us)
Async XLA Ops:
  0.6 9.6 %copy-start.10 = (f32[4,3,512]{2,0,1:T(4,128)S(1)}, f32[4,3,512]{2,0,1:T(4,128)}, u32[]{:S(2)}) copy-start(f32[4,3,512]{2,0,1:T(4,128)} %param.18) | copy-start | bytes 73732
  0.6 9.6 %copy-start.11 = (f32[4,3,512]{2,0,1:T(4,128)S(1)}, f32[4,3,512]{2,0,1:T(4,128)}, u32[]{:S(2)}) copy-start(f32[4,3,512]{2,0,1:T(4,128)} %param.17) | copy-start | bytes 73732
  6.7 9.5 %copy-start.13 = (bf16[4,2048,512]{2,1,0:T(8,128)(2,1)S(1)}, bf16[4,2048,512]{2,1,0:T(8,128)(2,1)}, u32[]{:S(2)}) copy-start(bf16[4,2048,512]{2,1,0:T(8,128)(2,1)} %param.16) | copy-start | bytes 25165828
  10.4 10.8 %copy-start.14 = (bf16[4,2048,512]{2,1,0:T(8,128)(2,1)S(1)}, bf16[4,2048,512]{2,1,0:T(8,128)(2,1)}, u32[]{:S(2)}) copy-start(bf16[4,2048,512]{2,1,0:T(8,128)(2,1)} %param.15) | copy-start | bytes 25165828
  77.9 18.0 %slice-start = ((s8[25165824]{0:T(1024)(128)(4,1)}), s8[4194304]{0:T(1024)(128)(4,1)S(1)}, s32[]{:S(2)}) async-start(s8[25165824]{0:T(1024)(128)(4,1)} %bitcast.340), calls=%async_computation | async-start | bytes 8388608
  78.0 18.0 %slice-start.1 = ((s8[25165824]{0:T(1024)(128)(4,1)}), s8[4194304]{0:T(1024)(128)(4,1)S(1)}, s32[]{:S(2)}) async-start(s8[25165824]{0:T(1024)(128)(4,1)} %bitcast.340), calls=%async_computation.1 | async-start | bytes 8388608
  78.0 18.0 %slice-start.2 = ((s8[25165824]{0:T(1024)(128)(4,1)}), s8[4194304]{0:T(1024)(128)(4,1)S(1)}, s32[]{:S(2)}) async-start(s8[25165824]{0:T(1024)(128)(4,1)} %bitcast.340), calls=%async_computation.2 | async-start | bytes 8388608
  87.0 9.0 %slice-start.3 = ((s8[25165824]{0:T(1024)(128)(4,1)}), s8[4194304]{0:T(1024)(128)(4,1)S(1)}, s32[]{:S(2)}) async-start(s8[25165824]{0:T(1024)(128)(4,1)} %bitcast.340), calls=%async_computation.3 | async-start | bytes 8388608
  87.0 9.0 %slice-start.4 = ((s8[25165824]{0:T(1024)(128)(4,1)}), s8[4194304]{0:T(1024)(128)(4,1)S(1)}, s32[]{:S(2)}) async-start(s8[25165824]{0:T(1024)(128)(4,1)} %bitcast.340), calls=%async_computation.4 | async-start | bytes 8388608
  87.0 9.0 %slice-start.5 = ((s8[25165824]{0:T(1024)(128)(4,1)}), s8[4194304]{0:T(1024)(128)(4,1)S(1)}, s32[]{:S(2)}) async-start(s8[25165824]{0:T(1024)(128)(4,1)} %bitcast.340), calls=%async_computation.5 | async-start | bytes 8388608
  103.1 35.1 %copy-start.9 = (f32[4,512]{1,0:T(4,128)S(1)}, f32[4,512]{1,0:T(4,128)}, u32[]{:S(2)}) copy-start(f32[4,512]{1,0:T(4,128)} %param.19) | copy-start | bytes 24580
  103.1 36.4 %copy-start.12 = (f32[4,512]{1,0:T(4,128)S(1)}, f32[4,512]{1,0:T(4,128)}, u32[]{:S(2)}) copy-start(f32[4,512]{1,0:T(4,128)} %param.20) | copy-start | bytes 24580
  203.7 1.7 copy-start.1
  253.0 6.5 %copy-start.5 = (f32[3,512,512]{2,1,0:T(8,128)S(1)}, f32[3,512,512]{2,1,0:T(8,128)}, u32[]{:S(2)}) copy-start(f32[3,512,512]{2,1,0:T(8,128)} %get-tuple-element.166) | copy-start | bytes 9437188
  256.6 5.1 %copy-start.7 = (f32[3,512,512]{2,1,0:T(8,128)S(1)}, f32[3,512,512]{2,1,0:T(8,128)}, u32[]{:S(2)}) copy-start(f32[3,512,512]{2,1,0:T(8,128)} %get-tuple-element.165) | copy-start | bytes 9437188
  259.4 3.0 copy-start.3
  296.9 4.9 %copy-start.2 = (f32[1,3,512,512]{2,3,1,0:T(8,128)S(1)}, f32[1,3,512,512]{2,3,1,0:T(8,128)}, u32[]{:S(2)}) copy-start(f32[1,3,512,512]{2,3,1,0:T(8,128)} %copy.61) | copy-start | bytes 9437188
  296.9 4.9 %copy-start.6 = (f32[3,512,512]{2,1,0:T(8,128)S(1)}, f32[3,512,512]{2,1,0:T(8,128)}, u32[]{:S(2)}) copy-start(f32[3,512,512]{2,1,0:T(8,128)} %get-tuple-element.166) | copy-start | bytes 9437188
  301.8 2.0 copy-start.8
  303.8 2.5 copy-start
  303.9 2.8 copy-start.4
where the time goes:
time: 331 us; the launch traced here: 325 us
  blocking collectives  160 us (48%)
  other arithmetic  57.1 us (17%)
  matrix products  45.4 us (14%)
  local copies, waits for them, and re-layouts  39.8 us (12%)
  between operations  23.2 us (7%)
    psum x2, blocking collectives, factored_step(): scalar_sum = lax.psum(scalar_part, (m_axis, n_axis))  67.8 us
    psum x2, blocking collectives, factored_step(): u_sum = lax.psum(jnp.sum(update * update, axis=(1, 2)), (m_axis, n_axis))  64.9 us
    dot_general x4, matrix products, local_run(): jnp.einsum('td,ktn->kdn', x_in[layer_idx], dy_qkv[layer_idx], preferred_e...  32.5 us
    unnamed x49, local copies, waits for them, and re-layouts  27.3 us
    another operation x14, other arithmetic, local_run(): jnp.stack([layer_out[out_slot] for layer_out in per_layer])  16.9 us
    psum x1, blocking collectives, factored_step(): row_sum = lax.psum(row_part, n_axis)  16.5 us
    dot_general x4, matrix products, local_run(): jnp.einsum('ti,td->id', x_attn[layer_idx], dy_out[layer_idx], preferred_e...  13 us
    psum x1, blocking collectives, factored_step(): col_sum = lax.psum(col_part, m_axis)  10.5 us

commit v1 on v0

v1 whole, which is shorter than its diff:
```python
import functools

import jax
import jax.numpy as jnp
from jax import lax
from jax.experimental import pallas as pl
from jax.experimental.pallas import tpu as pltpu
from jax.sharding import PartitionSpec as P

EPS_SQUARE = 1e-30
EPS_SCALE = 1e-3
MESH = pl.DeviceIdType.MESH
F32 = jnp.float32
BF16 = jnp.bfloat16
NA = 4
NE = 4
LAYERS = 4
MATS = 16
TOK = 2048
B = 512
LANES = 128
NDY = 5
NX = 3
KCH = 4
GROUPS = ((0, 4), (4, 4), (8, 4), (12, 2), (14, 1), (15, 1))


def col_of(row_piece):
    return jnp.broadcast_to(row_piece, (LANES, LANES)).T


def stats_body(
    n_total,
    w_qkv, w_out, x_in, dy_qkv, x_attn, dy_out, r_qkv, c_qkv, r_out, c_out, hyper,
    g, w, rq, cq, ro, co, bs,
    xbuf, dybuf, attbuf, embbuf, bbuf, rq_old, cq_old, ro_old, co_old, hp,
    xsem, dysem, wsem, insem, ch_sem, a_send, a_recv, e_send, e_recv, b_send, b_recv,
):
    a = lax.axis_index("att")
    e = lax.axis_index("emb")
    me = a * NE + e

    barrier = pltpu.get_barrier_semaphore()
    for da in range(NA):
        for de in range(NE):
            if da or de:
                pl.semaphore_signal(
                    barrier, inc=1, device_id=(lax.rem(a + da, NA), lax.rem(e + de, NE)), device_id_type=MESH
                )

    def x_copy(xi):
        l, kind = divmod(xi, 2)
        src = (x_attn if kind else x_in).at[l]
        return pltpu.make_async_copy(src, xbuf.at[xi % NX], xsem.at[xi % NX])

    def dy_copy(s):
        l, m = divmod(s, 4)
        src = dy_out.at[l] if m == 3 else dy_qkv.at[l, m]
        return pltpu.make_async_copy(src, dybuf.at[s % NDY], dysem.at[s % NDY])

    def w_copy(s):
        l, m = divmod(s, 4)
        src = w_out.at[l] if m == 3 else w_qkv.at[l, m]
        return pltpu.make_async_copy(src, w.at[s], wsem.at[s])

    def first_chunk(k):
        rows = pl.ds(k * (TOK // KCH), TOK // KCH)
        return (
            pltpu.make_async_copy(x_in.at[0, rows], xbuf.at[0, rows], ch_sem.at[2 * k]),
            pltpu.make_async_copy(dy_qkv.at[0, 0, rows], dybuf.at[0, rows], ch_sem.at[2 * k + 1]),
        )

    small = [
        pltpu.make_async_copy(r_qkv, rq_old, insem.at[0]),
        pltpu.make_async_copy(c_qkv, cq_old, insem.at[1]),
        pltpu.make_async_copy(r_out, ro_old, insem.at[2]),
        pltpu.make_async_copy(c_out, co_old, insem.at[3]),
        pltpu.make_async_copy(hyper, hp, insem.at[4]),
    ]

    for k in range(KCH):
        for c in first_chunk(k):
            c.start()
    dy_copy(1).start()
    dy_copy(2).start()
    for c in small:
        c.start()

    def stats(s):
        is_out = s % 4 == 3
        row_dst, row_me = (embbuf, e) if is_out else (attbuf, a)
        col_dst, col_me = (attbuf, a) if is_out else (embbuf, e)
        acc = [None] * 4
        for c in range(4):
            rows = pl.ds(c * LANES, LANES)
            lane_part = None
            for j in range(4):
                blk = g[s, rows, pl.ds(j * LANES, LANES)]
                sq = blk * blk
                lane_part = sq if lane_part is None else lane_part + sq
                part = jnp.sum(sq.reshape(LANES // 8, 8, LANES), axis=0)
                acc[j] = part if acc[j] is None else acc[j] + part
            row_dst[row_me, s, c : c + 1, :] = jnp.sum(lane_part.T, axis=0, keepdims=True)
        for j in range(4):
            col_dst[col_me, s, j : j + 1, :] = jnp.sum(acc[j], axis=0, keepdims=True)

    def a_copies(gi):
        s0, n = GROUPS[gi]
        sl = pl.ds(s0, n)
        out = []
        for d in range(1, NA):
            out.append(
                pltpu.make_async_remote_copy(
                    src_ref=attbuf.at[a, sl], dst_ref=attbuf.at[a, sl],
                    send_sem=a_send.at[gi, d], recv_sem=a_recv.at[gi, a],
                    device_id=(lax.rem(a + d, NA), e), device_id_type=MESH,
                )
            )
        for d in range(1, NE):
            out.append(
                pltpu.make_async_remote_copy(
                    src_ref=embbuf.at[e, sl], dst_ref=embbuf.at[e, sl],
                    send_sem=e_send.at[gi, d], recv_sem=e_recv.at[gi, e],
                    device_id=(a, lax.rem(e + d, NE)), device_id_type=MESH,
                )
            )
        return out

    def a_wait(gi):
        s0, n = GROUPS[gi]
        sl = pl.ds(s0, n)
        for d in range(1, NA):
            src = lax.rem(a + d, NA)
            pltpu.make_async_remote_copy(
                src_ref=attbuf.at[src, sl], dst_ref=attbuf.at[src, sl],
                send_sem=a_send.at[gi, d], recv_sem=a_recv.at[gi, src],
                device_id=(src, e), device_id_type=MESH,
            ).wait_recv()
        for d in range(1, NE):
            src = lax.rem(e + d, NE)
            pltpu.make_async_remote_copy(
                src_ref=embbuf.at[src, sl], dst_ref=embbuf.at[src, sl],
                send_sem=e_send.at[gi, d], recv_sem=e_recv.at[gi, src],
                device_id=(a, src), device_id_type=MESH,
            ).wait_recv()

    def b_copy(l, d, to):
        da, de = divmod(d, NE)
        if to:
            src = me
            dev = (lax.rem(a + da, NA), lax.rem(e + de, NE))
        else:
            dev = (lax.rem(a + da, NA), lax.rem(e + de, NE))
            src = dev[0] * NE + dev[1]
        return pltpu.make_async_remote_copy(
            src_ref=bbuf.at[l, src], dst_ref=bbuf.at[l, src],
            send_sem=b_send.at[l, d], recv_sem=b_recv.at[l, src],
            device_id=dev, device_id_type=MESH,
        )

    lane = lax.broadcasted_iota(jnp.int32, (1, LANES), 1)

    def finish(s):
        l, m = divmod(s, 4)
        is_out = m == 3
        row_src, col_src = (embbuf, attbuf) if is_out else (attbuf, embbuf)
        beta = hp[0]
        one_beta = 1.0 - beta
        acc = [None] * 4
        r_sum = None
        for c in range(4):
            ls = pl.ds(c * LANES, LANES)
            tot = (row_src[0, s, c : c + 1, :] + row_src[1, s, c : c + 1, :]) + (
                row_src[2, s, c : c + 1, :] + row_src[3, s, c : c + 1, :]
            )
            old = ro_old[l : l + 1, ls] if is_out else rq_old[m, l : l + 1, ls]
            r_new = beta * old + one_beta * (tot * (1.0 / n_total) + EPS_SQUARE)
            if is_out:
                ro[l : l + 1, ls] = r_new
            else:
                rq[m, l : l + 1, ls] = r_new
            r_sum = r_new if r_sum is None else r_sum + r_new
            factor = col_of(lax.rsqrt(r_new))
            for j in range(4):
                t = g[s, ls, pl.ds(j * LANES, LANES)] * factor
                part = jnp.sum((t * t).reshape(LANES // 8, 8, LANES), axis=0)
                acc[j] = part if acc[j] is None else acc[j] + part
        u = None
        for c in range(4):
            ls = pl.ds(c * LANES, LANES)
            tot = (col_src[0, s, c : c + 1, :] + col_src[1, s, c : c + 1, :]) + (
                col_src[2, s, c : c + 1, :] + col_src[3, s, c : c + 1, :]
            )
            old = co_old[l : l + 1, ls] if is_out else cq_old[m, l : l + 1, ls]
            c_new = beta * old + one_beta * (tot * (1.0 / n_total) + EPS_SQUARE)
            if is_out:
                co[l : l + 1, ls] = c_new
            else:
                cq[m, l : l + 1, ls] = c_new
            col_factor = lax.rsqrt(c_new)
            part = acc[c] * (col_factor * col_factor)
            u = part if u is None else u + part
        bbuf[l, me, m : m + 1, :] = jnp.sum(u, axis=0, keepdims=True)
        w_sum = wsq[s]
        bbuf[l, me, 4 + m : 5 + m, :] = jnp.where(
            lane < LANES // 2, w_sum + pltpu.roll(w_sum, LANES // 2, 1), r_sum + pltpu.roll(r_sum, LANES // 2, 1)
        )

    wsq = {}

    def w_square(s):
        w_copy(s).wait()
        acc = None
        for c in range(4):
            for j in range(4):
                blk = w[s, pl.ds(c * LANES, LANES), pl.ds(j * LANES, LANES)]
                part = jnp.sum((blk * blk).reshape(LANES // 8, 8, LANES), axis=0)
                acc = part if acc is None else acc + part
        wsq[s] = jnp.sum(acc, axis=0, keepdims=True)

    DN = (((0,), (0,)), ((), ()))
    for s in range(MATS):
        l, m = divmod(s, 4)
        xi = 2 * l + (m == 3)
        if s + 3 < MATS:
            nl, nm = divmod(s + 3, 4)
            if nm == 3 or nm == 0:
                x_copy(2 * nl + (nm == 3)).start()
            dy_copy(s + 3).start()
        w_copy(s).start()
        if s == 5:
            pl.semaphore_wait(barrier, NA * NE - 1)
        for gi, (s0, n) in enumerate(GROUPS):
            if s0 + n + 1 == s:
                for c in a_copies(gi):
                    c.start()
        todo = []
        if s == 1:
            for c in small:
                c.wait()
        if s in (7, 11, 15):
            a_wait((s - 7) // 4)
            todo = [s - 7, s - 6]
        if s in (8, 12):
            todo = [s - 6, s - 5]
        if s in (9, 13):
            for d in range(1, NA * NE):
                b_copy((s - 9) // 4, d, True).start()
        if s >= 2:
            w_copy_todo = [s - 2]
        else:
            w_copy_todo = []
        if s == 0:
            for k in range(KCH):
                rows = pl.ds(k * (TOK // KCH), TOK // KCH)
                for c in first_chunk(k):
                    c.wait()
                part = lax.dot_general(xbuf[0, rows], dybuf[0, rows], DN, preferred_element_type=F32)
                g[0] = part if k == 0 else g[0] + part
        else:
            if m == 0 or m == 3:
                x_copy(xi).wait()
            dy_copy(s).wait()
            g[s] = lax.dot_general(xbuf[xi % NX], dybuf[s % NDY], DN, preferred_element_type=F32)
        if s >= 1:
            stats(s - 1)
        for t in w_copy_todo:
            w_square(t)
        for t in todo:
            finish(t)

    for c in a_copies(4):
        c.start()
    stats(15)
    for c in a_copies(5):
        c.start()
    w_square(14)
    w_square(15)
    finish(10)
    finish(11)
    for d in range(1, NA * NE):
        b_copy(2, d, True).start()
    a_wait(3)
    finish(12)
    finish(13)
    a_wait(4)
    finish(14)
    a_wait(5)
    finish(15)
    for d in range(1, NA * NE):
        b_copy(3, d, True).start()
    for l in range(LAYERS):
        for d in range(1, NA * NE):
            b_copy(l, d, False).wait_recv()
        tot = bbuf[l, 0]
        for d in range(1, NA * NE):
            tot = tot + bbuf[l, d]
        bs[l] = tot
    for gi in range(len(GROUPS)):
        for c in a_copies(gi):
            c.wait_send()
    for l in range(LAYERS):
        for d in range(1, NA * NE):
            b_copy(l, d, True).wait_send()


NOUT = 4


def update_body(
    n_total, g, w, rq, cq, ro, co, bs, hyper,
    w_qkv_new, w_out_new, rq_new, cq_new, ro_new, co_new,
    obuf, hp, osem, rsem, hsem,
):
    load_hp = pltpu.make_async_copy(hyper, hp, hsem)
    load_hp.start()
    small = [
        pltpu.make_async_copy(rq, rq_new, rsem.at[0]),
        pltpu.make_async_copy(cq, cq_new, rsem.at[1]),
        pltpu.make_async_copy(ro, ro_new, rsem.at[2]),
        pltpu.make_async_copy(co, co_new, rsem.at[3]),
    ]
    for c in small:
        c.start()
    load_hp.wait()
    rho = hp[1]
    clip = hp[2]
    n_elems = float(n_total) * float(n_total)
    lane = lax.broadcasted_iota(jnp.int32, (1, LANES), 1)
    low = lane < LANES // 2

    def out_copy(s):
        l, m = divmod(s, 4)
        dst = w_out_new.at[l] if m == 3 else w_qkv_new.at[l, m]
        return pltpu.make_async_copy(obuf.at[s % NOUT], dst, osem.at[s % NOUT])

    for l in range(LAYERS):
        u_sum = jnp.sum(bs[l, 0:4, :], axis=1, keepdims=True)
        wr = bs[l, 4:8, :]
        w_sum = jnp.sum(jnp.where(low, wr, 0.0), axis=1, keepdims=True)
        r_mean = jnp.sum(jnp.where(low, 0.0, wr), axis=1, keepdims=True) * (0.25 / n_total)
        rms_u = jnp.sqrt(u_sum * r_mean / n_elems)
        rms_w = jnp.sqrt(w_sum / n_elems)
        step = rho * jnp.maximum(EPS_SCALE, rms_w) * jnp.sqrt(r_mean) / jnp.maximum(1.0, rms_u / clip)
        for m in range(4):
            s = 4 * l + m
            if s >= NOUT:
                out_copy(s - NOUT).wait()
            st = step[m : m + 1, :]
            cols = []
            for j in range(4):
                ls = pl.ds(j * LANES, LANES)
                c_new = co[l : l + 1, ls] if m == 3 else cq[m, l : l + 1, ls]
                cols.append(lax.rsqrt(c_new) * st)
            for c in range(4):
                ls = pl.ds(c * LANES, LANES)
                r_new = ro[l : l + 1, ls] if m == 3 else rq[m, l : l + 1, ls]
                factor = col_of(lax.rsqrt(r_new))
                for j in range(4):
                    js = pl.ds(j * LANES, LANES)
                    obuf[s % NOUT, ls, js] = w[s, ls, js] - (g[s, ls, js] * factor) * cols[j]
            out_copy(s).start()
    for s in range(MATS - NOUT, MATS):
        out_copy(s).wait()
    for c in small:
        c.wait()


def solution(mesh):
    in_specs = (
        P(None, None, "emb", "att"),
        P(None, "att", "emb"),
        P(None, None, "emb"),
        P(None, None, None, "att"),
        P(None, None, "att"),
        P(None, None, "emb"),
        P(None, None, "emb"),
        P(None, None, "att"),
        P(None, "att"),
        P(None, "emb"),
        P(),
    )
    out_specs = (
        P(None, None, "emb", "att"),
        P(None, "att", "emb"),
        P(None, None, "emb"),
        P(None, None, "att"),
        P(None, "att"),
        P(None, "emb"),
    )
    n_total = B * NA
    hbm = pl.BlockSpec(memory_space=pltpu.HBM)
    vm = pl.BlockSpec(memory_space=pltpu.VMEM)
    dma = pltpu.SemaphoreType.DMA

    def local_run(w_qkv, w_out, x_in, dy_qkv, x_attn, dy_out, r_qkv, c_qkv, r_out, c_out, hyper_params):
        ng = len(GROUPS)
        swap = lambda v: jnp.transpose(v, (1, 0, 2))
        mid = pl.pallas_call(
            functools.partial(stats_body, n_total),
            out_shape=(
                pltpu.VMEM((MATS, B, B), F32),
                pltpu.VMEM((MATS, B, B), F32),
                pltpu.VMEM((3, LAYERS, B), F32),
                pltpu.VMEM((3, LAYERS, B), F32),
                pltpu.VMEM((LAYERS, B), F32),
                pltpu.VMEM((LAYERS, B), F32),
                pltpu.VMEM((LAYERS, 8, LANES), F32),
            ),
            in_specs=[hbm] * 11,
            out_specs=(vm,) * 7,
            scratch_shapes=[
                pltpu.VMEM((NX, TOK, B), BF16),
                pltpu.VMEM((NDY, TOK, B), BF16),
                pltpu.VMEM((NA, MATS, 4, LANES), F32),
                pltpu.VMEM((NE, MATS, 4, LANES), F32),
                pltpu.VMEM((LAYERS, NA * NE, 8, LANES), F32),
                pltpu.VMEM((3, LAYERS, B), F32),
                pltpu.VMEM((3, LAYERS, B), F32),
                pltpu.VMEM((LAYERS, B), F32),
                pltpu.VMEM((LAYERS, B), F32),
                pltpu.SMEM((3,), F32),
                dma((NX,)),
                dma((NDY,)),
                dma((MATS,)),
                dma((5,)),
                dma((2 * KCH,)),
                dma((ng, NA)),
                dma((ng, NA)),
                dma((ng, NE)),
                dma((ng, NE)),
                dma((LAYERS, NA * NE)),
                dma((LAYERS, NA * NE)),
            ],
            compiler_params=pltpu.CompilerParams(
                collective_id=0, has_side_effects=True, vmem_limit_bytes=24 * 2**20
            ),
            name="stats",
        )(w_qkv, w_out, x_in, dy_qkv, x_attn, dy_out, swap(r_qkv), swap(c_qkv), r_out, c_out, hyper_params)
        new = pl.pallas_call(
            functools.partial(update_body, n_total),
            out_shape=(
                jax.ShapeDtypeStruct(w_qkv.shape, F32),
                jax.ShapeDtypeStruct(w_out.shape, F32),
                jax.ShapeDtypeStruct((3, LAYERS, B), F32),
                jax.ShapeDtypeStruct((3, LAYERS, B), F32),
                jax.ShapeDtypeStruct(r_out.shape, F32),
                jax.ShapeDtypeStruct(c_out.shape, F32),
            ),
            in_specs=[vm] * 7 + [hbm],
            out_specs=(hbm,) * 6,
            scratch_shapes=[
                pltpu.VMEM((NOUT, B, B), F32),
                pltpu.SMEM((3,), F32),
                dma((NOUT,)),
                dma((4,)),
                dma,
            ],
            compiler_params=pltpu.CompilerParams(vmem_limit_bytes=8 * 2**20),
            name="update",
        )(*mid, hyper_params)
        return new[0], new[1], swap(new[2]), swap(new[3]), new[4], new[5]

    return jax.shard_map(local_run, mesh=mesh, in_specs=in_specs, out_specs=out_specs, check_vma=False)
```

time: 331 us -> 70.3 us (0.21); the launches traced: 325 us -> 70.1 us
  blocking collectives: 160 us -> 0 us
  other arithmetic: 57.1 us -> 0 us
  Pallas kernels: 0 us -> 46.3 us
  matrix products: 45.4 us -> 0 us
  between operations: 23.2 us -> 0.82 us
  local copies, waits for them, and re-layouts: 39.8 us -> 23 us
    psum x6 -> x0, blocking collectives: 160 us -> none  [the longest x2 67.8 us: factored_step(): scalar_sum = lax.psum(scalar_part, (m_axis, n_axis))]
    pallas_call x0 -> x2, Pallas kernels: none -> 46.3 us  [the longest x1 39.6 us: local_run(): pl.pallas_call(functools.partial(stats_body, n_total), out_shape=(pltpu.V...]
    dot_general x8 -> x0, matrix products: 45.4 us -> none  [the longest x4 32.5 us: local_run(): jnp.einsum('td,ktn->kdn', x_in[layer_idx], dy_qkv[layer_idx], preferred_e...]
    another operation x22 -> x0, other arithmetic: 22.3 us -> none  [the longest x14 16.9 us: local_run(): jnp.stack([layer_out[out_slot] for layer_out in per_layer])]
    reduce_sum x15 -> x0, other arithmetic: 20.5 us -> none  [the longest x8 9.91 us: factored_step(): u_sum = lax.psum(jnp.sum(update * update, axis=(1, 2)), (m_axis, n_axis))]
    slice x5 -> x0, local copies, waits for them, and re-layouts: 12.5 us -> none  [the longest x1 9.75 us: local_run(): w_qkv[layer_idx]]
    div x8 -> x0, other arithmetic: 8.83 us -> none  [the longest x4 5.92 us: factored_step(): rel_step * jnp.maximum(EPS_SCALE, rms_w)]
    unnamed x49 -> x10, local copies, waits for them, and re-layouts: 27.3 us -> 23 us
where the time goes in v1:
time: 70.3 us; the launch traced here: 70.1 us
  Pallas kernels  46.3 us (66%)
  local copies, waits for them, and re-layouts  23 us (33%)
  between operations  0.82 us (1%)
    pallas_call x1, Pallas kernels, local_run(): pl.pallas_call(functools.partial(stats_body, n_total), out_shape=(pltpu.V...  39.6 us
    unnamed x10, local copies, waits for them, and re-layouts  23 us
    pallas_call x1, Pallas kernels, local_run(): pl.pallas_call(functools.partial(update_body, n_total), out_shape=(jax.Sh...  6.67 us

profile of v1, /device:TPU:0, one launch (start us, length us, event | category | flops | bytes accessed | tf_op | source)
XLA Modules:
  0.0 70.1 jit_solution(3295056744352748444)
XLA Ops:
  0.6 0.0 copy-start.4
  0.6 39.6 %stats.1 = (f32[16,512,512]{2,1,0:T(8,128)S(1)}, f32[16,512,512]{2,1,0:T(8,128)S(1)}, f32[3,4,512]{2,1,0:T(4,128)S(1)}, f32[3,4,512]{2,1,0:T(4,128)S(1)}, f32[4,...) custom-call(f32[4,3,512,512]{3,2,1,0:T(8,128)} %w_qkv.1, f32[4,512,512]{2,1,0:T(8,128)} %w_out.1, ...), custom_call_target="tpu_custom_call" | custom-call | tf_op jit(solution)/shard_map/stats/pallas_call | solution.py:399
  40.3 0.0 copy-start
  40.3 5.7 %copy-done = f32[16,512,512]{2,1,0:T(8,128)} copy-done((f32[16,512,512]{2,1,0:T(8,128)}, f32[16,512,512]{2,1,0:T(8,128)S(1)}, u32[]{:S(2)}) %copy-start) | copy-done | bytes 16777240
  46.0 0.0 copy-start.2
  46.0 5.7 %copy-done.2 = f32[16,512,512]{2,1,0:T(8,128)} copy-done((f32[16,512,512]{2,1,0:T(8,128)}, f32[16,512,512]{2,1,0:T(8,128)S(1)}, u32[]{:S(2)}) %copy-start.2) | copy-done | bytes 16777240
  51.8 0.0 copy-done.4
  51.8 0.0 copy-start.1
  51.8 5.8 %copy-done.1 = f32[16,512,512]{2,1,0:T(8,128)S(1)} copy-done((f32[16,512,512]{2,1,0:T(8,128)S(1)}, f32[16,512,512]{2,1,0:T(8,128)}, u32[]{:S(2)}) %copy-start.1) | copy-done | bytes 16777240
  57.5 0.0 copy-start.3
  57.5 5.8 %copy-done.3 = f32[16,512,512]{2,1,0:T(8,128)S(1)} copy-done((f32[16,512,512]{2,1,0:T(8,128)S(1)}, f32[16,512,512]{2,1,0:T(8,128)}, u32[]{:S(2)}) %copy-start.3) | copy-done | bytes 16777240
  63.3 6.7 %update.1 = (f32[4,3,512,512]{3,2,1,0:T(8,128)}, f32[4,512,512]{2,1,0:T(8,128)}, f32[3,4,512]{2,1,0:T(4,128)}, f32[3,4,512]{2,1,0:T(4,128)}, f32[4,512]{1,0:T(4,128)}, /*index=5*/f32[4,512]{1,0:T(4,128)}) custom-call(f32[16,512,512]{2,1,0:T(8,128)S(1)} %copy-done.1, f32[16,512,512]{2,1,0:T(8,128)S(1)} %copy-done.3, f32[3,4,512]{2,1,0:T(4,128)S(1)} %get-tuple-element.21.rq, ...), custom_call_target="tpu_custom_call" | custom-call | tf_op jit(solution)/shard_map/update/pallas_call | solution.py:440
Async XLA Ops:
  0.6 51.1 %copy-start.4 = (f32[3]{0:T(128)S(1)}, f32[3]{0:T(128)}, u32[]{:S(2)}) copy-start(f32[3]{0:T(128)} %hyper.3) | copy-start | bytes 40
  40.3 5.7 %copy-start = (f32[16,512,512]{2,1,0:T(8,128)}, f32[16,512,512]{2,1,0:T(8,128)S(1)}, u32[]{:S(2)}) copy-start(f32[16,512,512]{2,1,0:T(8,128)S(1)} %get-tuple-element.19.g) | copy-start | bytes 50331652
  46.0 5.7 %copy-start.2 = (f32[16,512,512]{2,1,0:T(8,128)}, f32[16,512,512]{2,1,0:T(8,128)S(1)}, u32[]{:S(2)}) copy-start(f32[16,512,512]{2,1,0:T(8,128)S(1)} %get-tuple-element.20.w) | copy-start | bytes 50331652
  51.8 5.8 %copy-start.1 = (f32[16,512,512]{2,1,0:T(8,128)S(1)}, f32[16,512,512]{2,1,0:T(8,128)}, u32[]{:S(2)}) copy-start(f32[16,512,512]{2,1,0:T(8,128)} %copy-done) | copy-start | bytes 50331652
  57.5 5.8 %copy-start.3 = (f32[16,512,512]{2,1,0:T(8,128)S(1)}, f32[16,512,512]{2,1,0:T(8,128)}, u32[]{:S(2)}) copy-start(f32[16,512,512]{2,1,0:T(8,128)} %copy-done.2) | copy-start | bytes 50331652

commit v2 on v1

--- a/solution.py
+++ b/solution.py
@@ -22,18 +22,47 @@
 NDY = 5
 NX = 3
 KCH = 4
+LAST = 12
+NG = 12
 GROUPS = ((0, 4), (4, 4), (8, 4), (12, 2), (14, 1), (15, 1))
+
+
+A_WAIT = {7: 0, 11: 1, 15: 2}
+B_SEND = {9: 0, 13: 1}
+FINISHES = {0: 7, 1: 7, 2: 8, 3: 8, 4: 11, 5: 11, 6: 12, 7: 12, 8: 15, 9: 15, 10: 15, 11: 15}
+UPDATES = {0: 11, 1: 12, 2: 13, 3: 13, 4: 15, 5: 15, 6: 15, 7: 15}
 
 
 def col_of(row_piece):
     return jnp.broadcast_to(row_piece, (LANES, LANES)).T
+
+
+def step_sizes(tot, n_total, rho, clip):
+    n_elems = float(n_total) * float(n_total)
+    low = lax.broadcasted_iota(jnp.int32, (1, LANES), 1) < LANES // 2
+    u_sum = jnp.sum(tot[0:4, :], axis=1, keepdims=True)
+    w_sum = jnp.sum(jnp.where(low, tot[4:8, :], 0.0), axis=1, keepdims=True)
+    r_mean = jnp.sum(jnp.where(low, 0.0, tot[4:8, :]), axis=1, keepdims=True) * (0.25 / n_total)
+    rms_u = jnp.sqrt(u_sum * r_mean / n_elems)
+    rms_w = jnp.sqrt(w_sum / n_elems)
+    return rho * jnp.maximum(EPS_SCALE, rms_w) * jnp.sqrt(r_mean) / jnp.maximum(1.0, rms_u / clip)
+
+
+def update_one(dst, w_ref, g_ref, row_pieces, col_pieces, st):
+    cols = [lax.rsqrt(c_new) * st for c_new in col_pieces]
+    for c in range(4):
+        ls = pl.ds(c * LANES, LANES)
+        factor = col_of(lax.rsqrt(row_pieces[c]))
+        for j in range(4):
+            js = pl.ds(j * LANES, LANES)
+            dst[ls, js] = w_ref[ls, js] - (g_ref[ls, js] * factor) * cols[j]
 
 
 def stats_body(
     n_total,
     w_qkv, w_out, x_in, dy_qkv, x_attn, dy_out, r_qkv, c_qkv, r_out, c_out, hyper,
-    g, w, rq, cq, ro, co, bs,
-    xbuf, dybuf, attbuf, embbuf, bbuf, rq_old, cq_old, ro_old, co_old, hp,
+    wn, g3, w3, rq, cq, ro, co, bs,
+    xbuf, dybuf, attbuf, embbuf, bbuf, rq_old, cq_old, ro_old, co_old, hp, gring,
     xsem, dysem, wsem, insem, ch_sem, a_send, a_recv, e_send, e_recv, b_send, b_recv,
 ):
     a = lax.axis_index("att")
@@ -48,6 +77,12 @@
                     barrier, inc=1, device_id=(lax.rem(a + da, NA), lax.rem(e + de, NE)), device_id_type=MESH
                 )
 
+    def g_at(s):
+        return g3.at[s - LAST] if s >= LAST else gring.at[s % NG]
+
+    def w_at(s):
+        return w3.at[s - LAST] if s >= LAST else wn.at[s]
+
     def x_copy(xi):
         l, kind = divmod(xi, 2)
         src = (x_attn if kind else x_in).at[l]
@@ -61,7 +96,7 @@
     def w_copy(s):
         l, m = divmod(s, 4)
         src = w_out.at[l] if m == 3 else w_qkv.at[l, m]
-        return pltpu.make_async_copy(src, w.at[s], wsem.at[s])
+        return pltpu.make_async_copy(src, w_at(s), wsem.at[s])
 
     def first_chunk(k):
         rows = pl.ds(k * (TOK // KCH), TOK // KCH)
@@ -95,7 +130,7 @@
             rows = pl.ds(c * LANES, LANES)
             lane_part = None
             for j in range(4):
-                blk = g[s, rows, pl.ds(j * LANES, LANES)]
+                blk = g_at(s)[rows, pl.ds(j * LANES, LANES)]
                 sq = blk * blk
                 lane_part = sq if lane_part is None else lane_part + sq
                 part = jnp.sum(sq.reshape(LANES // 8, 8, LANES), axis=0)
@@ -182,7 +217,7 @@
             r_sum = r_new if r_sum is None else r_sum + r_new
             factor = col_of(lax.rsqrt(r_new))
             for j in range(4):
-                t = g[s, ls, pl.ds(j * LANES, LANES)] * factor
+                t = g_at(s)[ls, pl.ds(j * LANES, LANES)] * factor
                 part = jnp.sum((t * t).reshape(LANES // 8, 8, LANES), axis=0)
                 acc[j] = part if acc[j] is None else acc[j] + part
         u = None
@@ -206,6 +241,30 @@
             lane < LANES // 2, w_sum + pltpu.roll(w_sum, LANES // 2, 1), r_sum + pltpu.roll(r_sum, LANES // 2, 1)
         )
 
+    def pieces(s):
+        l, m = divmod(s, 4)
+        sl = [pl.ds(c * LANES, LANES) for c in range(4)]
+        if m == 3:
+            return [ro[l : l + 1, i] for i in sl], [co[l : l + 1, i] for i in sl]
+        return [rq[m, l : l + 1, i] for i in sl], [cq[m, l : l + 1, i] for i in sl]
+
+    steps = {}
+
+    def gather_b(l):
+        for d in range(1, NA * NE):
+            b_copy(l, d, False).wait_recv()
+        tot = bbuf[l, 0]
+        for d in range(1, NA * NE):
+            tot = tot + bbuf[l, d]
+        return tot
+
+    def update(s):
+        l, m = divmod(s, 4)
+        if l not in steps:
+            steps[l] = step_sizes(gather_b(l), n_total, hp[1], hp[2])
+        rows, cols = pieces(s)
+        update_one(wn.at[s], wn.at[s], g_at(s), rows, cols, steps[l][m : m + 1, :])
+
     wsq = {}
 
     def w_square(s):
@@ -213,7 +272,7 @@
         acc = None
         for c in range(4):
             for j in range(4):
-                blk = w[s, pl.ds(c * LANES, LANES), pl.ds(j * LANES, LANES)]
+                blk = w_at(s)[pl.ds(c * LANES, LANES), pl.ds(j * LANES, LANES)]
                 part = jnp.sum((blk * blk).reshape(LANES // 8, 8, LANES), axis=0)
                 acc = part if acc is None else acc + part
         wsq[s] = jnp.sum(acc, axis=0, keepdims=True)
@@ -234,52 +293,48 @@
             if s0 + n + 1 == s:
                 for c in a_copies(gi):
                     c.start()
-        todo = []
         if s == 1:
             for c in small:
                 c.wait()
-        if s in (7, 11, 15):
-            a_wait((s - 7) // 4)
-            todo = [s - 7, s - 6]
-        if s in (8, 12):
-            todo = [s - 6, s - 5]
-        if s in (9, 13):
+        if s in A_WAIT:
+            a_wait(A_WAIT[s])
+        if s in B_SEND:
             for d in range(1, NA * NE):
-                b_copy((s - 9) // 4, d, True).start()
-        if s >= 2:
-            w_copy_todo = [s - 2]
-        else:
-            w_copy_todo = []
+                b_copy(B_SEND[s], d, True).start()
+        ups = [t for t, at in UPDATES.items() if at == s]
+        if ups and ups[0] // 4 not in steps:
+            steps[ups[0] // 4] = step_sizes(gather_b(ups[0] // 4), n_total, hp[1], hp[2])
         if s == 0:
             for k in range(KCH):
                 rows = pl.ds(k * (TOK // KCH), TOK // KCH)
                 for c in first_chunk(k):
                     c.wait()
                 part = lax.dot_general(xbuf[0, rows], dybuf[0, rows], DN, preferred_element_type=F32)
-                g[0] = part if k == 0 else g[0] + part
+                g_at(0)[...] = part if k == 0 else g_at(0)[...] + part
         else:
             if m == 0 or m == 3:
                 x_copy(xi).wait()
             dy_copy(s).wait()
-            g[s] = lax.dot_general(xbuf[xi % NX], dybuf[s % NDY], DN, preferred_element_type=F32)
+            g_at(s)[...] = lax.dot_general(xbuf[xi % NX], dybuf[s % NDY], DN, preferred_element_type=F32)
         if s >= 1:
             stats(s - 1)
-        for t in w_copy_todo:
-            w_square(t)
-        for t in todo:
-            finish(t)
+        if s >= 2:
+            w_square(s - 2)
+        for t, at in FINISHES.items():
+            if at == s:
+                finish(t)
+        for t in ups:
+            update(t)
 
     for c in a_copies(4):
         c.start()
     stats(15)
     for c in a_copies(5):
         c.start()
+    for d in range(1, NA * NE):
+        b_copy(2, d, True).start()
     w_square(14)
     w_square(15)
-    finish(10)
-    finish(11)
-    for d in range(1, NA * NE):
-        b_copy(2, d, True).start()
     a_wait(3)
     finish(12)
     finish(13)
@@ -289,13 +344,9 @@
     finish(15)
     for d in range(1, NA * NE):
         b_copy(3, d, True).start()
-    for l in range(LAYERS):
-        for d in range(1, NA * NE):
-            b_copy(l, d, False).wait_recv()
-        tot = bbuf[l, 0]
-        for d in range(1, NA * NE):
-            tot = tot + bbuf[l, d]
-        bs[l] = tot
+    for t in (8, 9, 10, 11):
+        update(t)
+    bs[...] = gather_b(3)
     for gi in range(len(GROUPS)):
         for c in a_copies(gi):
             c.wait_send()
@@ -304,16 +355,21 @@
             b_copy(l, d, True).wait_send()
 
 
-NOUT = 4
-
-
 def update_body(
-    n_total, g, w, rq, cq, ro, co, bs, hyper,
+    n_total, wn, g3, w3, rq, cq, ro, co, bs, hyper,
     w_qkv_new, w_out_new, rq_new, cq_new, ro_new, co_new,
     obuf, hp, osem, rsem, hsem,
 ):
     load_hp = pltpu.make_async_copy(hyper, hp, hsem)
     load_hp.start()
+
+    def out_copy(s):
+        l, m = divmod(s, 4)
+        dst = w_out_new.at[l] if m == 3 else w_qkv_new.at[l, m]
+        return pltpu.make_async_copy(obuf.at[s - LAST] if s >= LAST else wn.at[s], dst, osem.at[s])
+
+    for s in range(LAST):
+        out_copy(s).start()
     small = [
         pltpu.make_async_copy(rq, rq_new, rsem.at[0]),
         pltpu.make_async_copy(cq, cq_new, rsem.at[1]),
@@ -323,44 +379,17 @@
     for c in small:
         c.start()
     load_hp.wait()
-    rho = hp[1]
-    clip = hp[2]
-    n_elems = float(n_total) * float(n_total)
-    lane = lax.broadcasted_iota(jnp.int32, (1, LANES), 1)
-    low = lane < LANES // 2
-
-    def out_copy(s):
-        l, m = divmod(s, 4)
-        dst = w_out_new.at[l] if m == 3 else w_qkv_new.at[l, m]
-        return pltpu.make_async_copy(obuf.at[s % NOUT], dst, osem.at[s % NOUT])
-
-    for l in range(LAYERS):
-        u_sum = jnp.sum(bs[l, 0:4, :], axis=1, keepdims=True)
-        wr = bs[l, 4:8, :]
-        w_sum = jnp.sum(jnp.where(low, wr, 0.0), axis=1, keepdims=True)
-        r_mean = jnp.sum(jnp.where(low, 0.0, wr), axis=1, keepdims=True) * (0.25 / n_total)
-        rms_u = jnp.sqrt(u_sum * r_mean / n_elems)
-        rms_w = jnp.sqrt(w_sum / n_elems)
-        step = rho * jnp.maximum(EPS_SCALE, rms_w) * jnp.sqrt(r_mean) / jnp.maximum(1.0, rms_u / clip)
-        for m in range(4):
-            s = 4 * l + m
-            if s >= NOUT:
-                out_copy(s - NOUT).wait()
-            st = step[m : m + 1, :]
-            cols = []
-            for j in range(4):
-                ls = pl.ds(j * LANES, LANES)
-                c_new = co[l : l + 1, ls] if m == 3 else cq[m, l : l + 1, ls]
-                cols.append(lax.rsqrt(c_new) * st)
-            for c in range(4):
-                ls = pl.ds(c * LANES, LANES)
-                r_new = ro[l : l + 1, ls] if m == 3 else rq[m, l : l + 1, ls]
-                factor = col_of(lax.rsqrt(r_new))
-                for j in range(4):
-                    js = pl.ds(j * LANES, LANES)
-                    obuf[s % NOUT, ls, js] = w[s, ls, js] - (g[s, ls, js] * factor) * cols[j]
-            out_copy(s).start()
-    for s in range(MATS - NOUT, MATS):
+    l = LAYERS - 1
+    step = step_sizes(bs[...], n_total, hp[1], hp[2])
+    sl = [pl.ds(c * LANES, LANES) for c in range(4)]
+    for m in range(4):
+        if m == 3:
+            rows, cols = [ro[l : l + 1, i] for i in sl], [co[l : l + 1, i] for i in sl]
+        else:
+            rows, cols = [rq[m, l : l + 1, i] for i in sl], [cq[m, l : l + 1, i] for i in sl]
+        update_one(obuf.at[m], w3.at[m], g3.at[m], rows, cols, step[m : m + 1, :])
+        out_copy(LAST + m).start()
+    for s in range(MATS):
         out_copy(s).wait()
     for c in small:
         c.wait()
@@ -399,16 +428,17 @@
         mid = pl.pallas_call(
             functools.partial(stats_body, n_total),
             out_shape=(
-                pltpu.VMEM((MATS, B, B), F32),
-                pltpu.VMEM((MATS, B, B), F32),
+                pltpu.VMEM((LAST, B, B), F32),
+                pltpu.VMEM((4, B, B), F32),
+                pltpu.VMEM((4, B, B), F32),
                 pltpu.VMEM((3, LAYERS, B), F32),
                 pltpu.VMEM((3, LAYERS, B), F32),
                 pltpu.VMEM((LAYERS, B), F32),
                 pltpu.VMEM((LAYERS, B), F32),
-                pltpu.VMEM((LAYERS, 8, LANES), F32),
+                pltpu.VMEM((8, LANES), F32),
             ),
             in_specs=[hbm] * 11,
-            out_specs=(vm,) * 7,
+            out_specs=(vm,) * 8,
             scratch_shapes=[
                 pltpu.VMEM((NX, TOK, B), BF16),
                 pltpu.VMEM((NDY, TOK, B), BF16),
@@ -420,6 +450,7 @@
                 pltpu.VMEM((LAYERS, B), F32),
                 pltpu.VMEM((LAYERS, B), F32),
                 pltpu.SMEM((3,), F32),
+                pltpu.VMEM((NG, B, B), F32),
                 dma((NX,)),
                 dma((NDY,)),
                 dma((MATS,)),
@@ -433,7 +464,7 @@
                 dma((LAYERS, NA * NE)),
             ],
             compiler_params=pltpu.CompilerParams(
-                collective_id=0, has_side_effects=True, vmem_limit_bytes=24 * 2**20
+                collective_id=0, has_side_effects=True, vmem_limit_bytes=36 * 2**20
             ),
             name="stats",
         )(w_qkv, w_out, x_in, dy_qkv, x_attn, dy_out, swap(r_qkv), swap(c_qkv), r_out, c_out, hyper_params)
@@ -447,16 +478,16 @@
                 jax.ShapeDtypeStruct(r_out.shape, F32),
                 jax.ShapeDtypeStruct(c_out.shape, F32),
             ),
-            in_specs=[vm] * 7 + [hbm],
+            in_specs=[vm] * 8 + [hbm],
             out_specs=(hbm,) * 6,
             scratch_shapes=[
-                pltpu.VMEM((NOUT, B, B), F32),
+                pltpu.VMEM((4, B, B), F32),
                 pltpu.SMEM((3,), F32),
-                dma((NOUT,)),
+                dma((MATS,)),
                 dma((4,)),
                 dma,
             ],
-            compiler_params=pltpu.CompilerParams(vmem_limit_bytes=8 * 2**20),
+            compiler_params=pltpu.CompilerParams(vmem_limit_bytes=6 * 2**20),
             name="update",
         )(*mid, hyper_params)
         return new[0], new[1], swap(new[2]), swap(new[3]), new[4], new[5]

time: 70.3 us -> 48.9 us (0.70)
  local copies, waits for them, and re-layouts: 23 us -> 0.01 us
  Pallas kernels: 46.3 us -> 48 us
    unnamed x10 -> x2, local copies, waits for them, and re-layouts: 23 us -> 0.01 us
    pallas_call x1, Pallas kernels: 39.6 us -> 41.9 us  [local_run(): pl.pallas_call(functools.partial(stats_body, n_total), out_shape=(pltpu.V...]
where the time goes in v2:
time: 48.9 us; the launch traced here: 48.8 us
  Pallas kernels  48 us (98%)
  between operations  0.82 us (2%)
    pallas_call x1, Pallas kernels, local_run(): pl.pallas_call(functools.partial(stats_body, n_total), out_shape=(pltpu.V...  41.9 us
    pallas_call x1, Pallas kernels, local_run(): pl.pallas_call(functools.partial(update_body, n_total), out_shape=(jax.Sh...  6.04 us

profile of v2, /device:TPU:0, one launch (start us, length us, event | category | flops | bytes accessed | tf_op | source)
XLA Modules:
  0.0 48.8 jit_solution(4357468684058391907)
XLA Ops:
  0.6 0.0 copy-start
  0.6 41.9 %stats.1 = (f32[12,512,512]{2,1,0:T(8,128)S(1)}, f32[4,512,512]{2,1,0:T(8,128)S(1)}, f32[4,512,512]{2,1,0:T(8,128)S(1)}, f32[3,4,512]{2,1,0:T(4,128)S(1)}, f32[3...) custom-call(f32[4,3,512,512]{3,2,1,0:T(8,128)} %w_qkv.1, ...), custom_call_target="tpu_custom_call" | custom-call | tf_op jit(solution)/shard_map/stats/pallas_call | solution.py:428
  42.6 0.0 copy-done
  42.6 6.0 %update.1 = (f32[4,3,512,512]{3,2,1,0:T(8,128)}, f32[4,512,512]{2,1,0:T(8,128)}, f32[3,4,512]{2,1,0:T(4,128)}, f32[3,4,512]{2,1,0:T(4,128)}, f32[4,512]{1,0:T(4,128)}, /*index=5*/f32[4,512]{1,0:T(4,128)}) custom-call(f32[12,512,512]{2,1,0:T(8,128)S(1)} %get-tuple-element.20.wn, f32[4,512,512]{2,1,0:T(8,128)S(1)} %get-tuple-element.21.g3, ...), custom_call_target="tpu_custom_call" | custom-call | tf_op jit(solution)/shard_map/update/pallas_call | solution.py:471
Async XLA Ops:
  0.6 42.0 %copy-start = (f32[3]{0:T(128)S(1)}, f32[3]{0:T(128)}, u32[]{:S(2)}) copy-start(f32[3]{0:T(128)} %hyper.3) | copy-start | bytes 40

commit v3 on v2

--- a/solution.py
+++ b/solution.py
@@ -21,16 +21,16 @@
 LANES = 128
 NDY = 5
 NX = 3
+NW = 4
 KCH = 4
 LAST = 12
 NG = 12
 GROUPS = ((0, 4), (4, 4), (8, 4), (12, 2), (14, 1), (15, 1))
 
 
-A_WAIT = {7: 0, 11: 1, 15: 2}
-B_SEND = {9: 0, 13: 1}
-FINISHES = {0: 7, 1: 7, 2: 8, 3: 8, 4: 11, 5: 11, 6: 12, 7: 12, 8: 15, 9: 15, 10: 15, 11: 15}
-UPDATES = {0: 11, 1: 12, 2: 13, 3: 13, 4: 15, 5: 15, 6: 15, 7: 15}
+A_WAIT = {8: 0, 12: 1}
+B_SEND = {12: 0}
+FINISHES = {t: t + 8 for t in range(8)}
 
 
 def col_of(row_piece):
@@ -63,7 +63,7 @@
     w_qkv, w_out, x_in, dy_qkv, x_attn, dy_out, r_qkv, c_qkv, r_out, c_out, hyper,
     wn, g3, w3, rq, cq, ro, co, bs,
     xbuf, dybuf, attbuf, embbuf, bbuf, rq_old, cq_old, ro_old, co_old, hp, gring,
-    xsem, dysem, wsem, insem, ch_sem, a_send, a_recv, e_send, e_recv, b_send, b_recv,
+    xsem, dysem, wsem, insem, ch_sem, send_sem, a_recv, e_recv, b_recv,
 ):
     a = lax.axis_index("att")
     e = lax.axis_index("emb")
@@ -96,7 +96,7 @@
     def w_copy(s):
         l, m = divmod(s, 4)
         src = w_out.at[l] if m == 3 else w_qkv.at[l, m]
-        return pltpu.make_async_copy(src, w_at(s), wsem.at[s])
+        return pltpu.make_async_copy(src, w_at(s), wsem.at[s % NW])
 
     def first_chunk(k):
         rows = pl.ds(k * (TOK // KCH), TOK // KCH)
@@ -147,51 +147,35 @@
             out.append(
                 pltpu.make_async_remote_copy(
                     src_ref=attbuf.at[a, sl], dst_ref=attbuf.at[a, sl],
-                    send_sem=a_send.at[gi, d], recv_sem=a_recv.at[gi, a],
+                    send_sem=send_sem.at[0], recv_sem=a_recv.at[gi],
                     device_id=(lax.rem(a + d, NA), e), device_id_type=MESH,
                 )
             )
-        for d in range(1, NE):
             out.append(
                 pltpu.make_async_remote_copy(
                     src_ref=embbuf.at[e, sl], dst_ref=embbuf.at[e, sl],
-                    send_sem=e_send.at[gi, d], recv_sem=e_recv.at[gi, e],
+                    send_sem=send_sem.at[1], recv_sem=e_recv.at[gi],
                     device_id=(a, lax.rem(e + d, NE)), device_id_type=MESH,
                 )
             )
         return out
 
+    def wait_bytes(ref, sem):
+        pltpu.make_async_copy(ref, ref, sem).wait()
+
     def a_wait(gi):
         s0, n = GROUPS[gi]
-        sl = pl.ds(s0, n)
-        for d in range(1, NA):
-            src = lax.rem(a + d, NA)
+        wait_bytes(attbuf.at[pl.ds(0, NA - 1), pl.ds(s0, n)], a_recv.at[gi])
+        wait_bytes(embbuf.at[pl.ds(0, NE - 1), pl.ds(s0, n)], e_recv.at[gi])
+
+    def send_b(l):
+        for d in range(1, NA * NE):
+            da, de = divmod(d, NE)
             pltpu.make_async_remote_copy(
-                src_ref=attbuf.at[src, sl], dst_ref=attbuf.at[src, sl],
-                send_sem=a_send.at[gi, d], recv_sem=a_recv.at[gi, src],
-                device_id=(src, e), device_id_type=MESH,
-            ).wait_recv()
-        for d in range(1, NE):
-            src = lax.rem(e + d, NE)
-            pltpu.make_async_remote_copy(
-                src_ref=embbuf.at[src, sl], dst_ref=embbuf.at[src, sl],
-                send_sem=e_send.at[gi, d], recv_sem=e_recv.at[gi, src],
-                device_id=(a, src), device_id_type=MESH,
-            ).wait_recv()
-
-    def b_copy(l, d, to):
-        da, de = divmod(d, NE)
-        if to:
-            src = me
-            dev = (lax.rem(a + da, NA), lax.rem(e + de, NE))
-        else:
-            dev = (lax.rem(a + da, NA), lax.rem(e + de, NE))
-            src = dev[0] * NE + dev[1]
-        return pltpu.make_async_remote_copy(
-            src_ref=bbuf.at[l, src], dst_ref=bbuf.at[l, src],
-            send_sem=b_send.at[l, d], recv_sem=b_recv.at[l, src],
-            device_id=dev, device_id_type=MESH,
-        )
+                src_ref=bbuf.at[l, me], dst_ref=bbuf.at[l, me],
+                send_sem=send_sem.at[2], recv_sem=b_recv.at[l],
+                device_id=(lax.rem(a + da, NA), lax.rem(e + de, NE)), device_id_type=MESH,
+            ).start()
 
     lane = lax.broadcasted_iota(jnp.int32, (1, LANES), 1)
 
@@ -251,8 +235,7 @@
     steps = {}
 
     def gather_b(l):
-        for d in range(1, NA * NE):
-            b_copy(l, d, False).wait_recv()
+        wait_bytes(bbuf.at[l, pl.ds(0, NA * NE - 1)], b_recv.at[l])
         tot = bbuf[l, 0]
         for d in range(1, NA * NE):
             tot = tot + bbuf[l, d]
@@ -293,17 +276,13 @@
             if s0 + n + 1 == s:
                 for c in a_copies(gi):
                     c.start()
-        if s == 1:
+        if s == 8:
             for c in small:
                 c.wait()
         if s in A_WAIT:
             a_wait(A_WAIT[s])
         if s in B_SEND:
-            for d in range(1, NA * NE):
-                b_copy(B_SEND[s], d, True).start()
-        ups = [t for t, at in UPDATES.items() if at == s]
-        if ups and ups[0] // 4 not in steps:
-            steps[ups[0] // 4] = step_sizes(gather_b(ups[0] // 4), n_total, hp[1], hp[2])
+            send_b(B_SEND[s])
         if s == 0:
             for k in range(KCH):
                 rows = pl.ds(k * (TOK // KCH), TOK // KCH)
@@ -323,36 +302,34 @@
         for t, at in FINISHES.items():
             if at == s:
                 finish(t)
-        for t in ups:
-            update(t)
-
     for c in a_copies(4):
         c.start()
+    send_b(1)
     stats(15)
     for c in a_copies(5):
         c.start()
-    for d in range(1, NA * NE):
-        b_copy(2, d, True).start()
     w_square(14)
     w_square(15)
+    a_wait(2)
+    for t in (8, 9, 10, 11):
+        finish(t)
+    send_b(2)
     a_wait(3)
     finish(12)
     finish(13)
+    for t in (0, 1, 2, 3):
+        update(t)
     a_wait(4)
     finish(14)
     a_wait(5)
     finish(15)
-    for d in range(1, NA * NE):
-        b_copy(3, d, True).start()
-    for t in (8, 9, 10, 11):
+    send_b(3)
+    for t in range(4, LAST):
         update(t)
     bs[...] = gather_b(3)
-    for gi in range(len(GROUPS)):
-        for c in a_copies(gi):
-            c.wait_send()
-    for l in range(LAYERS):
-        for d in range(1, NA * NE):
-            b_copy(l, d, True).wait_send()
+    wait_bytes(attbuf.at[pl.ds(0, NA - 1)], send_sem.at[0])
+    wait_bytes(embbuf.at[pl.ds(0, NE - 1)], send_sem.at[1])
+    wait_bytes(bbuf.at[:, pl.ds(0, NA * NE - 1)], send_sem.at[2])
 
 
 def update_body(
@@ -366,7 +343,7 @@
     def out_copy(s):
         l, m = divmod(s, 4)
         dst = w_out_new.at[l] if m == 3 else w_qkv_new.at[l, m]
-        return pltpu.make_async_copy(obuf.at[s - LAST] if s >= LAST else wn.at[s], dst, osem.at[s])
+        return pltpu.make_async_copy(obuf.at[s - LAST] if s >= LAST else wn.at[s], dst, osem.at[m // 3 if s < LAST else s - LAST + 2])
 
     for s in range(LAST):
         out_copy(s).start()
@@ -389,7 +366,11 @@
             rows, cols = [rq[m, l : l + 1, i] for i in sl], [cq[m, l : l + 1, i] for i in sl]
         update_one(obuf.at[m], w3.at[m], g3.at[m], rows, cols, step[m : m + 1, :])
         out_copy(LAST + m).start()
-    for s in range(MATS):
+    first = w_qkv_new.at[pl.ds(0, LAYERS - 1)]
+    pltpu.make_async_copy(first, first, osem.at[0]).wait()
+    first = w_out_new.at[pl.ds(0, LAYERS - 1)]
+    pltpu.make_async_copy(first, first, osem.at[1]).wait()
+    for s in range(LAST, MATS):
         out_copy(s).wait()
     for c in small:
         c.wait()
@@ -453,15 +434,13 @@
                 pltpu.VMEM((NG, B, B), F32),
                 dma((NX,)),
                 dma((NDY,)),
-                dma((MATS,)),
+                dma((NW,)),
                 dma((5,)),
                 dma((2 * KCH,)),
-                dma((ng, NA)),
-                dma((ng, NA)),
-                dma((ng, NE)),
-                dma((ng, NE)),
-                dma((LAYERS, NA * NE)),
-                dma((LAYERS, NA * NE)),
+                dma((3,)),
+                dma((ng,)),
+                dma((ng,)),
+                dma((LAYERS,)),
             ],
             compiler_params=pltpu.CompilerParams(
                 collective_id=0, has_side_effects=True, vmem_limit_bytes=36 * 2**20
@@ -483,7 +462,7 @@
             scratch_shapes=[
                 pltpu.VMEM((4, B, B), F32),
                 pltpu.SMEM((3,), F32),
-                dma((MATS,)),
+                dma((6,)),
                 dma((4,)),
                 dma,
             ],

time: 48.9 us -> 42.6 us (0.87)
  Pallas kernels: 48 us -> 41.7 us
    pallas_call x1, Pallas kernels: 41.9 us -> 35.8 us  [local_run(): pl.pallas_call(functools.partial(stats_body, n_total), out_shape=(pltpu.V...]
where the time goes in v3:
time: 42.6 us; the launch traced here: 42.5 us
  Pallas kernels  41.7 us (98%)
  between operations  0.82 us (2%)
    pallas_call x1, Pallas kernels, local_run(): pl.pallas_call(functools.partial(stats_body, n_total), out_shape=(pltpu.V...  35.8 us
    pallas_call x1, Pallas kernels, local_run(): pl.pallas_call(functools.partial(update_body, n_total), out_shape=(jax.Sh...  5.95 us

profile of v3, /device:TPU:0, one launch (start us, length us, event | category | flops | bytes accessed | tf_op | source)
XLA Modules:
  0.0 42.5 jit_solution(3533172699265469199)
XLA Ops:
  0.6 0.0 copy-start
  0.6 35.8 %stats.1 = (f32[12,512,512]{2,1,0:T(8,128)S(1)}, f32[4,512,512]{2,1,0:T(8,128)S(1)}, f32[4,512,512]{2,1,0:T(8,128)S(1)}, f32[3,4,512]{2,1,0:T(4,128)S(1)}, f32[3...) custom-call(f32[4,3,512,512]{3,2,1,0:T(8,128)} %w_qkv.1, ...), custom_call_target="tpu_custom_call" | custom-call | tf_op jit(solution)/shard_map/stats/pallas_call | solution.py:409
  36.4 0.0 copy-done
  36.4 5.9 %update.1 = (f32[4,3,512,512]{3,2,1,0:T(8,128)}, f32[4,512,512]{2,1,0:T(8,128)}, f32[3,4,512]{2,1,0:T(4,128)}, f32[3,4,512]{2,1,0:T(4,128)}, f32[4,512]{1,0:T(4,128)}, /*index=5*/f32[4,512]{1,0:T(4,128)}) custom-call(f32[12,512,512]{2,1,0:T(8,128)S(1)} %get-tuple-element.20.wn, f32[4,512,512]{2,1,0:T(8,128)S(1)} %get-tuple-element.21.g3, ...), custom_call_target="tpu_custom_call" | custom-call | tf_op jit(solution)/shard_map/update/pallas_call | solution.py:450
Async XLA Ops:
  0.6 35.8 %copy-start = (f32[3]{0:T(128)S(1)}, f32[3]{0:T(128)}, u32[]{:S(2)}) copy-start(f32[3]{0:T(128)} %hyper.3) | copy-start | bytes 40

commit v4 on v3

--- a/solution.py
+++ b/solution.py
@@ -19,18 +19,37 @@
 TOK = 2048
 B = 512
 LANES = 128
-NDY = 5
-NX = 3
-NW = 4
+NDY = 8
+NX = 5
+NW = 16
 KCH = 4
 LAST = 12
 NG = 12
-GROUPS = ((0, 4), (4, 4), (8, 4), (12, 2), (14, 1), (15, 1))
-
-
-A_WAIT = {8: 0, 12: 1}
-B_SEND = {12: 0}
-FINISHES = {t: t + 8 for t in range(8)}
+GROUPS = ((0, 4), (4, 4), (8, 4), (12, 3), (15, 1))
+
+
+SLOTS = ((0,), (1,), (2,), (3,), (4, 5), (6, 7), (8, 9, 10), (11, 12, 13), (14, 15))
+AHEAD = 7
+W_ASK = {6: 1, 7: 4, 8: 16}
+W_SQUARE = {8: 4}
+FIRST_SEND = 5
+A_SEND = {5: 0, 7: 1, 8: 2}
+A_WAIT = {7: 0, 8: 1}
+FINISHES = {7: (0, 1, 2, 3), 8: (4, 5, 6, 7)}
+TILES = ((0, 8), (8, 4), (12, 4))
+STRIDE = 8
+
+
+def place(s):
+    return (s - LAST, 3) if s >= LAST else divmod(s, 3)
+
+
+def x_index(s):
+    return s - 8 if s >= LAST else s // 3
+
+
+def new_x(s):
+    return s >= LAST or s % 3 == 0
 
 
 def col_of(row_piece):
@@ -39,11 +58,9 @@
 
 def step_sizes(tot, n_total, rho, clip):
     n_elems = float(n_total) * float(n_total)
-    low = lax.broadcasted_iota(jnp.int32, (1, LANES), 1) < LANES // 2
-    u_sum = jnp.sum(tot[0:4, :], axis=1, keepdims=True)
-    w_sum = jnp.sum(jnp.where(low, tot[4:8, :], 0.0), axis=1, keepdims=True)
-    r_mean = jnp.sum(jnp.where(low, 0.0, tot[4:8, :]), axis=1, keepdims=True) * (0.25 / n_total)
-    rms_u = jnp.sqrt(u_sum * r_mean / n_elems)
+    w_sum = pltpu.roll(tot, LANES - STRIDE, 1)
+    r_mean = pltpu.roll(tot, LANES - 2 * STRIDE, 1) * (0.25 / n_total)
+    rms_u = jnp.sqrt(tot * r_mean / n_elems)
     rms_w = jnp.sqrt(w_sum / n_elems)
     return rho * jnp.maximum(EPS_SCALE, rms_w) * jnp.sqrt(r_mean) / jnp.maximum(1.0, rms_u / clip)
 
@@ -84,17 +101,16 @@
         return w3.at[s - LAST] if s >= LAST else wn.at[s]
 
     def x_copy(xi):
-        l, kind = divmod(xi, 2)
-        src = (x_attn if kind else x_in).at[l]
+        src = x_attn.at[xi - LAYERS] if xi >= LAYERS else x_in.at[xi]
         return pltpu.make_async_copy(src, xbuf.at[xi % NX], xsem.at[xi % NX])
 
     def dy_copy(s):
-        l, m = divmod(s, 4)
+        l, m = place(s)
         src = dy_out.at[l] if m == 3 else dy_qkv.at[l, m]
         return pltpu.make_async_copy(src, dybuf.at[s % NDY], dysem.at[s % NDY])
 
     def w_copy(s):
-        l, m = divmod(s, 4)
+        l, m = place(s)
         src = w_out.at[l] if m == 3 else w_qkv.at[l, m]
         return pltpu.make_async_copy(src, w_at(s), wsem.at[s % NW])
 
@@ -122,7 +138,7 @@
         c.start()
 
     def stats(s):
-        is_out = s % 4 == 3
+        is_out = s >= LAST
         row_dst, row_me = (embbuf, e) if is_out else (attbuf, a)
         col_dst, col_me = (attbuf, a) if is_out else (embbuf, e)
         acc = [None] * 4
@@ -180,7 +196,7 @@
     lane = lax.broadcasted_iota(jnp.int32, (1, LANES), 1)
 
     def finish(s):
-        l, m = divmod(s, 4)
+        l, m = place(s)
         is_out = m == 3
         row_src, col_src = (embbuf, attbuf) if is_out else (attbuf, embbuf)
         beta = hp[0]
@@ -219,14 +235,22 @@
             col_factor = lax.rsqrt(c_new)
             part = acc[c] * (col_factor * col_factor)
             u = part if u is None else u + part
-        bbuf[l, me, m : m + 1, :] = jnp.sum(u, axis=0, keepdims=True)
-        w_sum = wsq[s]
-        bbuf[l, me, 4 + m : 5 + m, :] = jnp.where(
-            lane < LANES // 2, w_sum + pltpu.roll(w_sum, LANES // 2, 1), r_sum + pltpu.roll(r_sum, LANES // 2, 1)
-        )
+        u_sums[s] = jnp.sum(jnp.sum(u, axis=0, keepdims=True), axis=1, keepdims=True)
+        r_sums[s] = jnp.sum(r_sum, axis=1, keepdims=True)
+
+    u_sums, r_sums = {}, {}
+
+    def pack(l):
+        row = jnp.zeros((1, LANES), F32)
+        s0, n = TILES[l]
+        for k, sums in enumerate((u_sums, wsq, r_sums)):
+            for i in range(n):
+                row = jnp.where(lane == STRIDE * k + i, sums[s0 + i], row)
+        bbuf[l, me] = row
+        send_b(l)
 
     def pieces(s):
-        l, m = divmod(s, 4)
+        l, m = place(s)
         sl = [pl.ds(c * LANES, LANES) for c in range(4)]
         if m == 3:
             return [ro[l : l + 1, i] for i in sl], [co[l : l + 1, i] for i in sl]
@@ -242,91 +266,101 @@
         return tot
 
     def update(s):
-        l, m = divmod(s, 4)
+        l = 0 if s < TILES[1][0] else 1
+        m = s - TILES[l][0]
         if l not in steps:
             steps[l] = step_sizes(gather_b(l), n_total, hp[1], hp[2])
         rows, cols = pieces(s)
-        update_one(wn.at[s], wn.at[s], g_at(s), rows, cols, steps[l][m : m + 1, :])
+        update_one(wn.at[s], wn.at[s], g_at(s), rows, cols, steps[l][:, m : m + 1])
 
     wsq = {}
 
     def w_square(s):
-        w_copy(s).wait()
         acc = None
         for c in range(4):
             for j in range(4):
                 blk = w_at(s)[pl.ds(c * LANES, LANES), pl.ds(j * LANES, LANES)]
                 part = jnp.sum((blk * blk).reshape(LANES // 8, 8, LANES), axis=0)
                 acc = part if acc is None else acc + part
-        wsq[s] = jnp.sum(acc, axis=0, keepdims=True)
+        wsq[s] = jnp.sum(jnp.sum(acc, axis=0, keepdims=True), axis=1, keepdims=True)
 
     DN = (((0,), (0,)), ((), ()))
-    for s in range(MATS):
-        l, m = divmod(s, 4)
-        xi = 2 * l + (m == 3)
-        if s + 3 < MATS:
-            nl, nm = divmod(s + 3, 4)
-            if nm == 3 or nm == 0:
-                x_copy(2 * nl + (nm == 3)).start()
-            dy_copy(s + 3).start()
-        w_copy(s).start()
-        if s == 5:
+    asked = 3
+    w_asked = 0
+    squared = 0
+    for slot, dots in enumerate(SLOTS):
+        while asked < min(dots[0] + AHEAD, MATS):
+            if new_x(asked):
+                x_copy(x_index(asked)).start()
+            dy_copy(asked).start()
+            asked += 1
+        while w_asked < W_ASK.get(slot, 0):
+            w_copy(w_asked).start()
+            w_asked += 1
+        if slot == FIRST_SEND:
             pl.semaphore_wait(barrier, NA * NE - 1)
-        for gi, (s0, n) in enumerate(GROUPS):
-            if s0 + n + 1 == s:
-                for c in a_copies(gi):
-                    c.start()
-        if s == 8:
+        if slot in A_SEND:
+            for c in a_copies(A_SEND[slot]):
+                c.start()
+        w_ready = W_SQUARE.get(slot, 0)
+        if slot == 7:
             for c in small:
                 c.wait()
-        if s in A_WAIT:
-            a_wait(A_WAIT[s])
-        if s in B_SEND:
-            send_b(B_SEND[s])
-        if s == 0:
-            for k in range(KCH):
-                rows = pl.ds(k * (TOK // KCH), TOK // KCH)
-                for c in first_chunk(k):
-                    c.wait()
-                part = lax.dot_general(xbuf[0, rows], dybuf[0, rows], DN, preferred_element_type=F32)
-                g_at(0)[...] = part if k == 0 else g_at(0)[...] + part
-        else:
-            if m == 0 or m == 3:
-                x_copy(xi).wait()
-            dy_copy(s).wait()
-            g_at(s)[...] = lax.dot_general(xbuf[xi % NX], dybuf[s % NDY], DN, preferred_element_type=F32)
-        if s >= 1:
-            stats(s - 1)
-        if s >= 2:
-            w_square(s - 2)
-        for t, at in FINISHES.items():
-            if at == s:
-                finish(t)
+        if slot in A_WAIT:
+            a_wait(A_WAIT[slot])
+        for t in range(squared, w_ready):
+            w_copy(t).wait()
+        if slot:
+            for s in dots:
+                if new_x(s):
+                    x_copy(x_index(s)).wait()
+                dy_copy(s).wait()
+        for s in dots:
+            xi = x_index(s)
+            if s == 0:
+                for k in range(KCH):
+                    rows = pl.ds(k * (TOK // KCH), TOK // KCH)
+                    for c in first_chunk(k):
+                        c.wait()
+                    part = lax.dot_general(xbuf[0, rows], dybuf[0, rows], DN, preferred_element_type=F32)
+                    g_at(0)[...] = part if k == 0 else g_at(0)[...] + part
+            else:
+                g_at(s)[...] = lax.dot_general(xbuf[xi % NX], dybuf[s % NDY], DN, preferred_element_type=F32)
+                stats(s - 1)
+        for t in range(squared, w_ready):
+            w_square(t)
+        squared = max(squared, w_ready)
+        for t in FINISHES.get(slot, ()):
+            finish(t)
+
+    for c in a_copies(3):
+        c.start()
+    stats(15)
     for c in a_copies(4):
         c.start()
-    send_b(1)
-    stats(15)
-    for c in a_copies(5):
-        c.start()
-    w_square(14)
-    w_square(15)
+
+    def square_more(s0):
+        for t in range(s0, s0 + 4):
+            w_copy(t).wait()
+        for t in range(s0, s0 + 4):
+            w_square(t)
+
+    square_more(4)
+    pack(0)
     a_wait(2)
+    square_more(8)
     for t in (8, 9, 10, 11):
         finish(t)
-    send_b(2)
+    pack(1)
+    square_more(12)
     a_wait(3)
-    finish(12)
-    finish(13)
-    for t in (0, 1, 2, 3):
+    a_wait(4)
+    for t in (12, 13, 14, 15):
+        finish(t)
+    pack(2)
+    for t in range(LAST):
         update(t)
-    a_wait(4)
-    finish(14)
-    a_wait(5)
-    finish(15)
-    send_b(3)
-    for t in range(4, LAST):
-        update(t)
-    bs[...] = gather_b(3)
+    bs[...] = gather_b(2)
     wait_bytes(attbuf.at[pl.ds(0, NA - 1)], send_sem.at[0])
     wait_bytes(embbuf.at[pl.ds(0, NE - 1)], send_sem.at[1])
     wait_bytes(bbuf.at[:, pl.ds(0, NA * NE - 1)], send_sem.at[2])
@@ -340,13 +374,11 @@
     load_hp = pltpu.make_async_copy(hyper, hp, hsem)
     load_hp.start()
 
-    def out_copy(s):
-        l, m = divmod(s, 4)
-        dst = w_out_new.at[l] if m == 3 else w_qkv_new.at[l, m]
-        return pltpu.make_async_copy(obuf.at[s - LAST] if s >= LAST else wn.at[s], dst, osem.at[m // 3 if s < LAST else s - LAST + 2])
-
+    first = []
     for s in range(LAST):
-        out_copy(s).start()
+        l, m = place(s)
+        first.append(pltpu.make_async_copy(wn.at[s], w_qkv_new.at[l, m], osem.at[0]))
+        first[-1].start()
     small = [
         pltpu.make_async_copy(rq, rq_new, rsem.at[0]),
         pltpu.make_async_copy(cq, cq_new, rsem.at[1]),
@@ -356,23 +388,16 @@
     for c in small:
         c.start()
     load_hp.wait()
-    l = LAYERS - 1
     step = step_sizes(bs[...], n_total, hp[1], hp[2])
     sl = [pl.ds(c * LANES, LANES) for c in range(4)]
-    for m in range(4):
-        if m == 3:
-            rows, cols = [ro[l : l + 1, i] for i in sl], [co[l : l + 1, i] for i in sl]
-        else:
-            rows, cols = [rq[m, l : l + 1, i] for i in sl], [cq[m, l : l + 1, i] for i in sl]
-        update_one(obuf.at[m], w3.at[m], g3.at[m], rows, cols, step[m : m + 1, :])
-        out_copy(LAST + m).start()
-    first = w_qkv_new.at[pl.ds(0, LAYERS - 1)]
-    pltpu.make_async_copy(first, first, osem.at[0]).wait()
-    first = w_out_new.at[pl.ds(0, LAYERS - 1)]
-    pltpu.make_async_copy(first, first, osem.at[1]).wait()
-    for s in range(LAST, MATS):
-        out_copy(s).wait()
-    for c in small:
+    last = []
+    for l in range(LAYERS):
+        rows, cols = [ro[l : l + 1, i] for i in sl], [co[l : l + 1, i] for i in sl]
+        update_one(obuf.at[l], w3.at[l], g3.at[l], rows, cols, step[:, l : l + 1])
+        last.append(pltpu.make_async_copy(obuf.at[l], w_out_new.at[l], osem.at[1 + l]))
+        last[-1].start()
+    pltpu.make_async_copy(w_qkv_new, w_qkv_new, osem.at[0]).wait()
+    for c in last + small:
         c.wait()
 
 
@@ -416,7 +441,7 @@
                 pltpu.VMEM((3, LAYERS, B), F32),
                 pltpu.VMEM((LAYERS, B), F32),
                 pltpu.VMEM((LAYERS, B), F32),
-                pltpu.VMEM((8, LANES), F32),
+                pltpu.VMEM((1, LANES), F32),
             ),
             in_specs=[hbm] * 11,
             out_specs=(vm,) * 8,
@@ -425,7 +450,7 @@
                 pltpu.VMEM((NDY, TOK, B), BF16),
                 pltpu.VMEM((NA, MATS, 4, LANES), F32),
                 pltpu.VMEM((NE, MATS, 4, LANES), F32),
-                pltpu.VMEM((LAYERS, NA * NE, 8, LANES), F32),
+                pltpu.VMEM((len(TILES), NA * NE, 1, LANES), F32),
                 pltpu.VMEM((3, LAYERS, B), F32),
                 pltpu.VMEM((3, LAYERS, B), F32),
                 pltpu.VMEM((LAYERS, B), F32),
@@ -440,10 +465,10 @@
                 dma((3,)),
                 dma((ng,)),
                 dma((ng,)),
-                dma((LAYERS,)),
+                dma((len(TILES),)),
             ],
             compiler_params=pltpu.CompilerParams(
-                collective_id=0, has_side_effects=True, vmem_limit_bytes=36 * 2**20
+                collective_id=0, has_side_effects=True, vmem_limit_bytes=42 * 2**20
             ),
             name="stats",
         )(w_qkv, w_out, x_in, dy_qkv, x_attn, dy_out, swap(r_qkv), swap(c_qkv), r_out, c_out, hyper_params)
@@ -462,7 +487,7 @@
             scratch_shapes=[
                 pltpu.VMEM((4, B, B), F32),
                 pltpu.SMEM((3,), F32),
-                dma((6,)),
+                dma((1 + LAYERS,)),
                 dma((4,)),
                 dma,
             ],

time: 42.6 us -> 38.8 us (0.911)
  Pallas kernels: 41.7 us -> 37.8 us
    pallas_call x1, Pallas kernels: 35.8 us -> 31.9 us  [local_run(): pl.pallas_call(functools.partial(stats_body, n_total), out_shape=(pltpu.V...]
where the time goes in v4:
time: 38.8 us; the launch traced here: 38.6 us
  Pallas kernels  37.8 us (97%)
  between operations  0.82 us (2%)
    pallas_call x1, Pallas kernels, local_run(): pl.pallas_call(functools.partial(stats_body, n_total), out_shape=(pltpu.V...  31.9 us
    pallas_call x1, Pallas kernels, local_run(): pl.pallas_call(functools.partial(update_body, n_total), out_shape=(jax.Sh...  5.94 us

profile of v4, /device:TPU:0, one launch (start us, length us, event | category | flops | bytes accessed | tf_op | source)
XLA Modules:
  0.0 38.6 jit_solution(2824597867295412797)
XLA Ops:
  0.6 0.0 copy-start
  0.6 31.9 %stats.1 = (f32[12,512,512]{2,1,0:T(8,128)S(1)}, f32[4,512,512]{2,1,0:T(8,128)S(1)}, f32[4,512,512]{2,1,0:T(8,128)S(1)}, f32[3,4,512]{2,1,0:T(4,128)S(1)}, f32[3...) custom-call(f32[4,3,512,512]{3,2,1,0:T(8,128)} %w_qkv.1, ...), custom_call_target="tpu_custom_call" | custom-call | tf_op jit(solution)/shard_map/stats/pallas_call | solution.py:434
  32.5 0.0 copy-done
  32.5 5.9 %update.1 = (f32[4,3,512,512]{3,2,1,0:T(8,128)}, f32[4,512,512]{2,1,0:T(8,128)}, f32[3,4,512]{2,1,0:T(4,128)}, f32[3,4,512]{2,1,0:T(4,128)}, f32[4,512]{1,0:T(4,128)}, /*index=5*/f32[4,512]{1,0:T(4,128)}) custom-call(f32[12,512,512]{2,1,0:T(8,128)S(1)} %get-tuple-element.20.wn, f32[4,512,512]{2,1,0:T(8,128)S(1)} %get-tuple-element.21.g3, ...), custom_call_target="tpu_custom_call" | custom-call | tf_op jit(solution)/shard_map/update/pallas_call | solution.py:475
Async XLA Ops:
  0.6 31.9 %copy-start = (f32[3]{0:T(128)S(1)}, f32[3]{0:T(128)}, u32[]{:S(2)}) copy-start(f32[3]{0:T(128)} %hyper.3) | copy-start | bytes 40

commit v5 on v4

--- a/solution.py
+++ b/solution.py
@@ -21,7 +21,7 @@
 LANES = 128
 NDY = 8
 NX = 5
-NW = 16
+NW = 4
 KCH = 4
 LAST = 12
 NG = 12
@@ -38,6 +38,7 @@
 FINISHES = {7: (0, 1, 2, 3), 8: (4, 5, 6, 7)}
 TILES = ((0, 8), (8, 4), (12, 4))
 STRIDE = 8
+FAR_FIRST = tuple((da, de) for da in (1, 3, 2, 0) for de in (1, 3, 2, 0) if da or de)
 
 
 def place(s):
@@ -112,13 +113,13 @@
     def w_copy(s):
         l, m = place(s)
         src = w_out.at[l] if m == 3 else w_qkv.at[l, m]
-        return pltpu.make_async_copy(src, w_at(s), wsem.at[s % NW])
+        return pltpu.make_async_copy(src, w_at(s), wsem.at[s // 4])
 
     def first_chunk(k):
         rows = pl.ds(k * (TOK // KCH), TOK // KCH)
         return (
-            pltpu.make_async_copy(x_in.at[0, rows], xbuf.at[0, rows], ch_sem.at[2 * k]),
-            pltpu.make_async_copy(dy_qkv.at[0, 0, rows], dybuf.at[0, rows], ch_sem.at[2 * k + 1]),
+            pltpu.make_async_copy(x_in.at[0, rows], xbuf.at[0, rows], ch_sem.at[k]),
+            pltpu.make_async_copy(dy_qkv.at[0, 0, rows], dybuf.at[0, rows], ch_sem.at[k]),
         )
 
     small = [
@@ -159,7 +160,7 @@
         s0, n = GROUPS[gi]
         sl = pl.ds(s0, n)
         out = []
-        for d in range(1, NA):
+        for d in (1, 3, 2):
             out.append(
                 pltpu.make_async_remote_copy(
                     src_ref=attbuf.at[a, sl], dst_ref=attbuf.at[a, sl],
@@ -185,8 +186,7 @@
         wait_bytes(embbuf.at[pl.ds(0, NE - 1), pl.ds(s0, n)], e_recv.at[gi])
 
     def send_b(l):
-        for d in range(1, NA * NE):
-            da, de = divmod(d, NE)
+        for da, de in FAR_FIRST:
             pltpu.make_async_remote_copy(
                 src_ref=bbuf.at[l, me], dst_ref=bbuf.at[l, me],
                 send_sem=send_sem.at[2], recv_sem=b_recv.at[l],
@@ -308,8 +308,8 @@
                 c.wait()
         if slot in A_WAIT:
             a_wait(A_WAIT[slot])
-        for t in range(squared, w_ready):
-            w_copy(t).wait()
+        if w_ready > squared:
+            wait_bytes(gring.at[pl.ds(0, 4)], wsem.at[0])
         if slot:
             for s in dots:
                 if new_x(s):
@@ -320,8 +320,7 @@
             if s == 0:
                 for k in range(KCH):
                     rows = pl.ds(k * (TOK // KCH), TOK // KCH)
-                    for c in first_chunk(k):
-                        c.wait()
+                    wait_bytes(xbuf.at[0, pl.ds(0, 2 * TOK // KCH)], ch_sem.at[k])
                     part = lax.dot_general(xbuf[0, rows], dybuf[0, rows], DN, preferred_element_type=F32)
                     g_at(0)[...] = part if k == 0 else g_at(0)[...] + part
             else:
@@ -340,8 +339,7 @@
         c.start()
 
     def square_more(s0):
-        for t in range(s0, s0 + 4):
-            w_copy(t).wait()
+        wait_bytes(gring.at[pl.ds(0, 4)], wsem.at[s0 // 4])
         for t in range(s0, s0 + 4):
             w_square(t)
 
@@ -461,7 +459,7 @@
                 dma((NDY,)),
                 dma((NW,)),
                 dma((5,)),
-                dma((2 * KCH,)),
+                dma((KCH,)),
                 dma((3,)),
                 dma((ng,)),
                 dma((ng,)),

time: 38.8 us -> 38.6 us (level)
  no operation moved by 1% of the time
where the time goes in v5:
time: 38.6 us; the launch traced here: 38.5 us
  Pallas kernels  37.6 us (97%)
  between operations  0.82 us (2%)
    pallas_call x1, Pallas kernels, local_run(): pl.pallas_call(functools.partial(stats_body, n_total), out_shape=(pltpu.V...  31.7 us
    pallas_call x1, Pallas kernels, local_run(): pl.pallas_call(functools.partial(update_body, n_total), out_shape=(jax.Sh...  5.94 us

profile of v5, /device:TPU:0, one launch (start us, length us, event | category | flops | bytes accessed | tf_op | source)
XLA Modules:
  0.0 38.5 jit_solution(1216809707928291044)
XLA Ops:
  0.6 0.0 copy-start
  0.6 31.7 %stats.1 = (f32[12,512,512]{2,1,0:T(8,128)S(1)}, f32[4,512,512]{2,1,0:T(8,128)S(1)}, f32[4,512,512]{2,1,0:T(8,128)S(1)}, f32[3,4,512]{2,1,0:T(4,128)S(1)}, f32[3...) custom-call(f32[4,3,512,512]{3,2,1,0:T(8,128)} %w_qkv.1, ...), custom_call_target="tpu_custom_call" | custom-call | tf_op jit(solution)/shard_map/stats/pallas_call | solution.py:432
  32.3 0.0 copy-done
  32.4 5.9 %update.1 = (f32[4,3,512,512]{3,2,1,0:T(8,128)}, f32[4,512,512]{2,1,0:T(8,128)}, f32[3,4,512]{2,1,0:T(4,128)}, f32[3,4,512]{2,1,0:T(4,128)}, f32[4,512]{1,0:T(4,128)}, /*index=5*/f32[4,512]{1,0:T(4,128)}) custom-call(f32[12,512,512]{2,1,0:T(8,128)S(1)} %get-tuple-element.20.wn, f32[4,512,512]{2,1,0:T(8,128)S(1)} %get-tuple-element.21.g3, ...), custom_call_target="tpu_custom_call" | custom-call | tf_op jit(solution)/shard_map/update/pallas_call | solution.py:473
Async XLA Ops:
  0.6 31.7 %copy-start = (f32[3]{0:T(128)S(1)}, f32[3]{0:T(128)}, u32[]{:S(2)}) copy-start(f32[3]{0:T(128)} %hyper.3) | copy-start | bytes 40
